TPU v7x, 32 devices: a whole 2x2x4 slice. The times are simulated.
32 devices in a mesh: tp: 32 (over z, y, x, core).
Axes of the slice: x: 2, y: 2, z: 4, core: 2. Of those that a mesh axis runs over, the one named last changes fastest.
Arguments:
- x_norm: bfloat16 [4096, 2048], P(None, 'tp')
- hid_act: bfloat16 [4096, 5120], P(None, 'tp')
- dy_in: bfloat16 [2, 4096, 5120], replicated
- dy_out: bfloat16 [4096, 2048], replicated
- w_in: float32 [2, 2048, 5120], P(None, 'tp')
- w_out: float32 [5120, 2048], P('tp')
- row_in: float32 [2, 2048], P(None, 'tp')
- col_in: float32 [2, 5120], replicated
- row_out: float32 [5120], P('tp')
- col_out: float32 [2048], replicated
- beta_two: float32 [], replicated
- rel_step: float32 [], replicated
- clip_rms: float32 [], replicated
- clip_norm: float32 [], replicated
Outputs:
- output 1: float32 [2, 2048, 5120], P(None, 'tp')
- output 2: float32 [2, 2048], P(None, 'tp')
- output 3: float32 [2, 5120], replicated
- output 4: float32 [5120, 2048], P('tp')
- output 5: float32 [5120], P('tp')
- output 6: float32 [2048], replicated
All inputs are finite; a program needn't handle non-finite values.
Results may differ from a plain program's by a relative error of at most 0.001.
Values are sent between devices in bfloat16 or wider.
A program may use at most 1 GiB of HBM per device.

v0:
```python
import jax
import jax.numpy as jnp
from jax import lax
from jax.sharding import PartitionSpec as P

EPS_ONE = 1e-30
EPS_TWO = 1e-3


def local_sums(gradient, weight, row_stat):
    col_sq = jnp.sum(gradient * gradient, axis=-2)
    row_sum = jnp.sum(row_stat, axis=-1, keepdims=True)
    w_sq = jnp.sum(weight * weight, axis=(-2, -1))[..., None]
    return jnp.concatenate([col_sq, row_sum, w_sq], axis=-1)


def apply_update(weight, gradient, row_stat, col_stat, totals, shards, beta_two, rel_step, clip_rms, grad_scale):
    rows_total = gradient.shape[-2] * shards
    col_count = gradient.shape[-1]
    col_sq = totals[..., :-2]
    row_sum = totals[..., -2:-1]
    w_sq = totals[..., -1:]
    mix_new = 1.0 - beta_two
    sq_scale = grad_scale * grad_scale
    scaled = grad_scale * gradient
    sq_grad = scaled * scaled + EPS_ONE
    row_new = beta_two * row_stat + mix_new * jnp.mean(sq_grad, axis=-1)
    col_new = beta_two * col_stat + mix_new * (sq_scale * col_sq / rows_total + EPS_ONE)
    grand_sum = jnp.sum(col_sq, axis=-1, keepdims=True)
    row_level = beta_two * row_sum / rows_total + mix_new * (sq_scale * grand_sum / (rows_total * col_count) + EPS_ONE)
    second = (row_new / row_level)[..., :, None] * col_new[..., None, :]
    update = scaled / jnp.sqrt(second)
    upd_sq = lax.psum(jnp.sum(update * update, axis=(-2, -1)), 'tp')
    upd_rms = jnp.sqrt(upd_sq / (rows_total * col_count))[..., None, None]
    clipped = update / jnp.maximum(1.0, upd_rms / clip_rms)
    w_rms = jnp.sqrt(w_sq / (rows_total * col_count))[..., None]
    step_size = rel_step * jnp.maximum(EPS_TWO, w_rms)
    return (weight - step_size * clipped, row_new, col_new)


def solution(mesh):
    shards = mesh.shape['tp']

    def local_step(x_norm, hid_act, dy_in, dy_out, w_in, w_out, row_in, col_in, row_out, col_out, beta_two, rel_step, clip_rms, clip_norm):
        grad_in = jnp.einsum('ti,ktj->kij', x_norm, dy_in, preferred_element_type=jnp.float32)
        grad_out = jnp.einsum('ti,tj->ij', hid_act, dy_out, preferred_element_type=jnp.float32)
        totals_in = lax.psum(local_sums(grad_in, w_in, row_in), 'tp')
        totals_out = lax.psum(local_sums(grad_out, w_out, row_out), 'tp')
        norm_sq = jnp.sum(totals_in[..., :-2]) + jnp.sum(totals_out[..., :-2])
        grad_scale = jnp.minimum(1.0, clip_norm / jnp.sqrt(norm_sq))
        new_in = apply_update(w_in, grad_in, row_in, col_in, totals_in, shards, beta_two, rel_step, clip_rms, grad_scale)
        new_out = apply_update(w_out, grad_out, row_out, col_out, totals_out, shards, beta_two, rel_step, clip_rms, grad_scale)
        return new_in + new_out

    in_specs = (P(None, 'tp'), P(None, 'tp'), P(), P(), P(None, 'tp', None), P('tp', None),
                P(None, 'tp'), P(), P('tp'), P(), P(), P(), P(), P())
    out_specs = (P(None, 'tp', None), P(None, 'tp'), P(), P('tp', None), P('tp'), P())
    return jax.shard_map(local_step, mesh=mesh, in_specs=in_specs, out_specs=out_specs, check_vma=False)
```

profile of v0, /device:TPU:0, one launch (start us, length us, event | category | flops | bytes accessed | tf_op | source)
XLA Modules:
  0.0 151.0 jit_solution(16253351322838303951)
XLA Ops:
  3.4 1.3 reduce_sum.126
  4.6 2.3 %multiply_reduce_fusion.4 = f32[]{:T(128)} fusion(f32[160,2048]{1,0:T(8,128)} %param.19), kind=kLoop, calls=%fused_computation.12 | loop fusion | flops 655359 | bytes 1310724 | tf_op jit(solution)/shard_map/reduce_sum | solution.py:13
  6.9 2.2 %multiply_reduce_fusion.1 = f32[2]{0:T(128)S(1)} fusion(f32[2,64,5120]{2,1,0:T(8,128)} %param.18), kind=kLoop, calls=%fused_computation.6 | loop fusion | flops 1310718 | bytes 2621448 | tf_op jit(solution)/shard_map/reduce_sum | solution.py:13
  9.1 0.1 copy.35
  9.2 0.1 reduce_sum.122
  9.3 0.1 copy.34
  9.4 7.4 %multiply_reduce_fusion.5 = (f32[2048]{0:T(1024)S(1)}, f32[160,2048]{1,0:T(8,128)S(1)}) fusion(bf16[4096,160]{0,1:T(8,128)(2,1)S(1)} %copy-done, bf16[4096,2048]{1,0:T(8,128)(2,1)} %param.17), kind=kOutput, calls=%fused_computation.13 | convolution fusion | flops 2685007872 | bytes 19406848 | tf_op jit(solution)/shard_map/ti,tj->ij/dot_general | solution.py:46
  16.8 1.4 concatenate.7
  18.2 30.6 %multiply_reduce_fusion.2 = (f32[2,5120]{1,0:T(2,128)S(1)}, f32[2,5120,64]{1,2,0:T(8,128)}) fusion(bf16[2,4096,5120]{2,1,0:T(8,128)(2,1)} %param.16, bf16[4096,64]{0,1:T(8,128)(2,1)S(1)} %copy-done.3), kind=kOutput, calls=%fused_computation.7 | convolution fusion | flops 5370009600 | bytes 87072768 | tf_op jit(solution)/shard_map/ti,ktj->kij/dot_general | solution.py:45
  48.8 0.1 concatenate.6
  48.9 42.6 %all-reduce.1 = (f32[2,5122]{1,0:T(2,128)S(1)}, f32[2050]{0:T(1024)S(1)}) all-reduce(f32[2,5122]{1,0:T(2,128)S(1)} %concatenate.6, f32[2050]{0:T(1024)S(1)} %concatenate.7), channel_id=1, replica_groups=mesh['tp'=32] {'tp'}, use_global_device_ids=true, to_apply=%region_3.0 | all-reduce | flops 12294 | bytes 98352 | tf_op jit(solution)/shard_map/psum | solution.py:47
  91.5 0.6 slice_reduce_fusion.2
  92.1 0.7 slice_reduce_fusion
  94.9 0.2 fusion.9
  95.2 0.3 add_reduce_fusion
  95.5 2.5 %fusion.1 = f32[2,64]{1,0:T(2,128)S(1)} fusion(f32[2,5120,64]{1,2,0:T(8,128)} %get-tuple-element.33, f32[]{:T(128)S(6)} %min.3), kind=kLoop, calls=%fused_computation.3 | loop fusion | flops 2621312 | bytes 2621956 | tf_op jit(solution)/shard_map/reduce_sum | solution.py:27
  97.9 0.6 broadcast_divide_fusion.1
  98.5 0.7 multiply_reduce_fusion
  99.2 0.6 fusion.11
  101.1 0.6 broadcast_divide_fusion
  101.7 1.2 multiply_reduce_fusion.3
  102.9 40.4 %all-reduce = (f32[2]{0:T(128)S(1)}, f32[]{:T(128)}) all-reduce(f32[2]{0:T(128)S(1)} %multiply_reduce_fusion, f32[]{:T(128)} %multiply_reduce_fusion.3), channel_id=1, replica_groups=mesh['tp'=32] {'tp'}, use_global_device_ids=true, to_apply=%region_13.0 | all-reduce | flops 3 | bytes 24 | tf_op jit(solution)/shard_map/psum | solution.py:33
  144.1 2.9 %multiply_subtract_fusion.1 = f32[160,2048]{1,0:T(8,128)} fusion(f32[160,2048]{1,0:T(8,128)} %param.19, f32[160,2048]{1,0:T(8,128)S(1)} %get-tuple-element.35, f32[]{:T(128)S(6)} %max.27, f32[2048]{0:T(1024)S(1)} %multiply_add_fusion.1, f32[160]{0:T(256)S(1)} %get-tuple-element.26, f32[]{:T(128)S(6)} %min.3, f32[]{:T(128)} %bitcast.9), kind=kLoop, calls=%fused_computation.8 | loop fusion | flops 1966080 | bytes 3941004 | tf_op jit(solution)/shard_map/sub | solution.py:38
  147.0 4.0 %multiply_subtract_fusion = f32[2,64,5120]{2,1,0:T(8,128)} fusion(f32[2,64,5120]{2,1,0:T(8,128)} %param.18, f32[2,5120,64]{1,2,0:T(8,128)S(1)} %copy-done.2, f32[2]{0:T(128)S(1)} %divide_maximum_fusion, f32[2,5120]{1,0:T(2,128)S(1)} %multiply_add_fusion, f32[2,64]{1,0:T(2,128)S(1)} %get-tuple-element.28, f32[]{:T(128)S(6)} %min.3, f32[2]{0:T(128)S(1)} %get-tuple-element.18), kind=kLoop, calls=%fused_computation.4 | loop fusion | flops 3932160 | bytes 7905812 | tf_op jit(solution)/shard_map/sub | solution.py:38
  (25 shorter events, 0.2 us)
Async XLA Ops:
  0.6 8.8 %copy-start = (bf16[4096,160]{0,1:T(8,128)(2,1)S(1)}, bf16[4096,160]{0,1:T(8,128)(2,1)}, u32[]{:S(2)}) copy-start(bf16[4096,160]{0,1:T(8,128)(2,1)} %param.15) | copy-start | bytes 3932164
  0.6 8.5 %copy-start.8 = (f32[2,64]{1,0:T(2,128)S(1)}, f32[2,64]{1,0:T(2,128)}, u32[]{:S(2)}) copy-start(f32[2,64]{1,0:T(2,128)} %param.20) | copy-start | bytes 1540
  9.4 8.8 %copy-start.3 = (bf16[4096,64]{0,1:T(8,128)(2,1)S(1)}, bf16[4096,64]{0,1:T(8,128)(2,1)}, u32[]{:S(2)}) copy-start(bf16[4096,64]{0,1:T(8,128)(2,1)} %param.14) | copy-start | bytes 1572868
  18.2 77.0 %copy-start.6 = (f32[2,5120]{1,0:T(2,128)S(1)}, f32[2,5120]{1,0:T(2,128)}, u32[]{:S(2)}) copy-start(f32[2,5120]{1,0:T(2,128)} %param.21) | copy-start | bytes 122884
  94.9 3.6 %copy-start.1 = (f32[2,5120,64]{1,2,0:T(8,128)S(1)}, f32[2,5120,64]{1,2,0:T(8,128)}, u32[]{:S(2)}) copy-start(f32[2,5120,64]{1,2,0:T(8,128)} %get-tuple-element.33) | copy-start | bytes 7864324
  95.2 51.8 %copy-start.4 = (f32[2,5120]{1,0:T(2,128)}, f32[2,5120]{1,0:T(2,128)S(1)}, u32[]{:S(2)}) copy-start(f32[2,5120]{1,0:T(2,128)S(1)} %multiply_add_fusion) | copy-start | bytes 122884
  95.4 5.6 %copy-start.7 = (f32[2048]{0:T(1024)S(1)}, f32[2048]{0:T(1024)}, u32[]{:S(2)}) copy-start(f32[2048]{0:T(1024)} %param.23) | copy-start | bytes 24580
  95.4 5.7 %copy-start.9 = (f32[160]{0:T(256)S(1)}, f32[160]{0:T(256)}, u32[]{:S(2)}) copy-start(f32[160]{0:T(256)} %param.22) | copy-start | bytes 1924
  101.1 45.9 %copy-start.5 = (f32[2048]{0:T(1024)}, f32[2048]{0:T(1024)S(1)}, u32[]{:S(2)}) copy-start(f32[2048]{0:T(1024)S(1)} %multiply_add_fusion.1) | copy-start | bytes 24580
  144.1 2.9 %copy-start.2 = (f32[2,5120,64]{1,2,0:T(8,128)S(1)}, f32[2,5120,64]{1,2,0:T(8,128)}, u32[]{:S(2)}) copy-start(f32[2,5120,64]{1,2,0:T(8,128)} %get-tuple-element.33) | copy-start | bytes 7864324
where the time goes:
time: 152 us; the launch traced here: 151 us
  blocking collectives  83 us (55%)
  matrix products  38 us (25%)
  other arithmetic  20.1 us (13%)
  between operations  7.47 us (5%)
  local copies, waits for them, and re-layouts  2.41 us (2%)
    psum x1, blocking collectives, local_step(): totals_in = lax.psum(local_sums(grad_in, w_in, row_in), 'tp')  42.6 us
    psum x1, blocking collectives, apply_update(): upd_sq = lax.psum(jnp.sum(update * update, axis=(-2, -1)), 'tp')  40.4 us
    dot_general x1, matrix products, local_step(): jnp.einsum('ti,ktj->kij', x_norm, dy_in, preferred_element_type=jnp.float32)  30.6 us
    dot_general x1, matrix products, local_step(): jnp.einsum('ti,tj->ij', hid_act, dy_out, preferred_element_type=jnp.float32)  7.39 us
    sub x2, other arithmetic, apply_update(): return (weight - step_size * clipped, row_new, col_new)  6.9 us
    reduce_sum x2, other arithmetic, local_sums(): w_sq = jnp.sum(weight * weight, axis=(-2, -1))[..., None]  4.43 us

commit v1 on v0

v1 whole, which is shorter than its diff:
```python
import jax
import jax.numpy as jnp
from jax import lax
from jax.experimental import pallas as pl
from jax.experimental.pallas import tpu as pltpu
from jax.sharding import PartitionSpec as P

EPS_ONE = 1e-30
EPS_TWO = 1e-3
LANES = 128


def peer_barrier(me, n):
    barrier = pltpu.get_barrier_semaphore()
    for d in range(1, n):
        pl.semaphore_signal(barrier, inc=1, device_id=(lax.rem(me + d, n),), device_id_type=pl.DeviceIdType.MESH)
    pl.semaphore_wait(barrier, n - 1)


def reduce_kernel(n, x_ref, out_ref, landed, owned, sems):
    me = lax.axis_index('tp')
    peer_barrier(me, n)

    def send(src, dst, phase):
        for d in range(1, n):
            peer = lax.rem(me + d, n)
            pltpu.make_async_remote_copy(src_ref=src(peer), dst_ref=dst, send_sem=sems.at[phase, 0], recv_sem=sems.at[phase, 1],
                                         device_id=(peer,), device_id_type=pl.DeviceIdType.MESH).start()

    def wait(side, phase):
        pltpu.make_async_copy(x_ref.at[pl.ds(0, n - 1)], landed.at[pl.ds(0, n - 1)], sems.at[phase, side]).wait()

    send(lambda peer: x_ref.at[peer], landed.at[me], 0)
    landed[me] = x_ref[me]
    wait(1, 0)
    total = jnp.sum(landed[...], axis=0)
    owned[...] = total
    out_ref[me] = total
    send(lambda peer: owned, out_ref.at[me], 1)
    wait(1, 1)
    wait(0, 0)
    wait(0, 1)


def all_sum(x, n):
    return pl.pallas_call(
        lambda *refs: reduce_kernel(n, *refs),
        out_shape=jax.ShapeDtypeStruct(x.shape, x.dtype),
        in_specs=[pl.BlockSpec(memory_space=pltpu.VMEM)],
        out_specs=pl.BlockSpec(memory_space=pltpu.VMEM),
        scratch_shapes=[pltpu.VMEM(x.shape, x.dtype), pltpu.VMEM(x.shape[1:], x.dtype), pltpu.SemaphoreType.DMA((2, 2))],
        compiler_params=pltpu.CompilerParams(collective_id=0, has_side_effects=True),
        name='all_sum',
    )(x)


def gather_kernel(n, x_ref, out_ref, landed, sems):
    me = lax.axis_index('tp')
    peer_barrier(me, n)
    for d in range(1, n):
        peer = lax.rem(me + d, n)
        pltpu.make_async_remote_copy(src_ref=x_ref, dst_ref=landed.at[me], send_sem=sems.at[0], recv_sem=sems.at[1],
                                     device_id=(peer,), device_id_type=pl.DeviceIdType.MESH).start()
    landed[me] = x_ref[...]
    pltpu.make_async_copy(landed.at[pl.ds(0, n - 1)], landed.at[pl.ds(0, n - 1)], sems.at[1]).wait()
    out_ref[...] = jnp.sum(landed[...], axis=0)
    pltpu.make_async_copy(landed.at[pl.ds(0, n - 1)], landed.at[pl.ds(0, n - 1)], sems.at[0]).wait()


def small_sum(x, n):
    return pl.pallas_call(
        lambda *refs: gather_kernel(n, *refs),
        out_shape=jax.ShapeDtypeStruct(x.shape, x.dtype),
        in_specs=[pl.BlockSpec(memory_space=pltpu.VMEM)],
        out_specs=pl.BlockSpec(memory_space=pltpu.VMEM),
        scratch_shapes=[pltpu.VMEM((n,) + x.shape, x.dtype), pltpu.SemaphoreType.DMA((2,))],
        compiler_params=pltpu.CompilerParams(collective_id=1, has_side_effects=True),
        name='small_sum',
    )(x)


def solution(mesh):
    shards = mesh.shape['tp']

    def local_step(x_norm, hid_act, dy_in, dy_out, w_in, w_out, row_in, col_in, row_out, col_out, beta_two, rel_step, clip_rms, clip_norm):
        grad_in = jnp.einsum('ti,ktj->kij', x_norm, dy_in, preferred_element_type=jnp.float32)
        grad_out = jnp.einsum('ti,tj->ij', hid_act, dy_out, preferred_element_type=jnp.float32)
        kinds, cols_in = grad_in.shape[0], grad_in.shape[2]
        cols_out = grad_out.shape[1]
        col_local = jnp.concatenate([jnp.sum(grad_in * grad_in, axis=1).reshape(-1), jnp.sum(grad_out * grad_out, axis=0)])
        scalars = jnp.concatenate([jnp.sum(row_in, axis=1), jnp.sum(row_out)[None],
                                   jnp.sum(w_in * w_in, axis=(1, 2)), jnp.sum(w_out * w_out)[None]])
        scalars = jnp.broadcast_to(jnp.pad(scalars, (0, LANES - 6)), (shards, 1, LANES))
        block = jnp.concatenate([col_local.reshape(shards, -1, LANES), scalars], axis=1)
        total = all_sum(block, shards)
        col_all = total[:, :-1].reshape(-1)
        sums = total[0, -1]
        grad_scale = jnp.minimum(1.0, clip_norm / jnp.sqrt(jnp.sum(col_all)))
        sq_scale = grad_scale * grad_scale
        mix_new = 1.0 - beta_two

        def stats(grad, row_stat, col_stat, col_sq, row_sum):
            rows_total, col_count = grad.shape[0] * shards, grad.shape[1]
            row_new = beta_two * row_stat + mix_new * (sq_scale * jnp.mean(grad * grad, axis=-1) + EPS_ONE)
            col_new = beta_two * col_stat + mix_new * (sq_scale * col_sq / rows_total + EPS_ONE)
            level = beta_two * row_sum / rows_total + mix_new * (sq_scale * jnp.sum(col_sq) / (rows_total * col_count) + EPS_ONE)
            update = (grad_scale * grad) * lax.rsqrt(row_new / level)[:, None] * lax.rsqrt(col_new)[None, :]
            return row_new, col_new, update, jnp.sum(update * update)

        parts = [stats(grad_in[k], row_in[k], col_in[k], col_all[k * cols_in:(k + 1) * cols_in], sums[k]) for k in range(kinds)]
        parts.append(stats(grad_out, row_out, col_out, col_all[kinds * cols_in:], sums[kinds]))
        upd = jnp.stack([p[3] for p in parts])
        upd = small_sum(jnp.broadcast_to(jnp.pad(upd, (0, LANES - 3)), (8, LANES)), shards)[0, :3]

        def apply(weight, update, k):
            count = weight.size * shards
            clip = jnp.maximum(1.0, jnp.sqrt(upd[k] / count) / clip_rms)
            step = rel_step * jnp.maximum(EPS_TWO, jnp.sqrt(sums[3 + k] / count))
            return weight - step * (update / clip)

        new_in = jnp.stack([apply(w_in[k], parts[k][2], k) for k in range(kinds)])
        new_out = apply(w_out, parts[2][2], 2)
        return (new_in, jnp.stack([parts[0][0], parts[1][0]]), jnp.stack([parts[0][1], parts[1][1]]),
                new_out, parts[2][0], parts[2][1])

    in_specs = (P(None, 'tp'), P(None, 'tp'), P(), P(), P(None, 'tp', None), P('tp', None),
                P(None, 'tp'), P(), P('tp'), P(), P(), P(), P(), P())
    out_specs = (P(None, 'tp', None), P(None, 'tp'), P(), P('tp', None), P('tp'), P())
    return jax.shard_map(local_step, mesh=mesh, in_specs=in_specs, out_specs=out_specs, check_vma=False)
```

time: 152 us -> 111 us (0.73)
  blocking collectives: 83 us -> 0 us
  Pallas kernels: 0 us -> 26.4 us
  other arithmetic: 20.1 us -> 26.4 us
  between operations: 7.47 us -> 12 us
  local copies, waits for them, and re-layouts: 2.41 us -> 5.26 us
  matrix products: 38 us -> 40.5 us
    psum x2 -> x0, blocking collectives: 83 us -> none  [the longest x1 42.6 us: local_step(): totals_in = lax.psum(local_sums(grad_in, w_in, row_in), 'tp')]
    pallas_call x0 -> x2, Pallas kernels: none -> 26.4 us  [the longest x1 17.8 us: all_sum(): pl.pallas_call(lambda *refs: reduce_kernel(n, *refs), out_shape=jax.Shape...]
    another operation x0 -> x4, other arithmetic: none -> 4.95 us  [the longest x1 2.05 us: local_step(): upd = jnp.stack([p[3] for p in parts])]
    rsqrt x0 -> x4, other arithmetic: none -> 2.4 us  [the longest x2 1.81 us: stats(): lax.rsqrt(col_new)[None, :]]
    dot_general x1, matrix products: 7.39 us -> 9.72 us  [local_step(): jnp.einsum('ti,tj->ij', hid_act, dy_out, preferred_element_type=jnp.float32)]
    slice x1 -> x2, local copies, waits for them, and re-layouts: 0.58 us -> 2.91 us  [the longest x1 1.52 us: apply(): step = rel_step * jnp.maximum(EPS_TWO, jnp.sqrt(sums[3 + k] / count))]
    concatenate x0 -> x3, other arithmetic: none -> 2.02 us  [the longest x1 1.37 us: local_step(): jnp.concatenate([jnp.sum(row_in, axis=1), jnp.sum(row_out)[None], jnp.sum...]
    unnamed x20 -> x17, local copies, waits for them, and re-layouts: 0.05 us -> 1.69 us
where the time goes in v1:
time: 111 us; the launch traced here: 110 us
  matrix products  40.5 us (36%)
  other arithmetic  26.4 us (24%)
  Pallas kernels  26.4 us (24%)
  between operations  12 us (11%)
  local copies, waits for them, and re-layouts  5.26 us (5%)
    dot_general x1, matrix products, local_step(): jnp.einsum('ti,ktj->kij', x_norm, dy_in, preferred_element_type=jnp.float32)  30.7 us
    pallas_call x1, Pallas kernels, all_sum(): pl.pallas_call(lambda *refs: reduce_kernel(n, *refs), out_shape=jax.Shape...  17.8 us
    dot_general x1, matrix products, local_step(): jnp.einsum('ti,tj->ij', hid_act, dy_out, preferred_element_type=jnp.float32)  9.72 us
    pallas_call x1, Pallas kernels, small_sum(): pl.pallas_call(lambda *refs: gather_kernel(n, *refs), out_shape=jax.Shape...  8.66 us
    sub x2, other arithmetic, apply(): return weight - step * (update / clip)  5.79 us
    reduce_sum x2, other arithmetic, stats(): return (row_new, col_new, update, jnp.sum(update * update))  3.7 us

profile of v1, /device:TPU:0, one launch (start us, length us, event | category | flops | bytes accessed | tf_op | source)
XLA Modules:
  0.0 110.5 jit_solution(6116009219695995336)
XLA Ops:
  0.7 1.3 %copy-done = bf16[4096,160]{0,1:T(8,128)(2,1)S(1)} copy-done((bf16[4096,160]{0,1:T(8,128)(2,1)S(1)}, bf16[4096,160]{0,1:T(8,128)(2,1)}, u32[]{:S(2)}) %copy-start) | copy-done | bytes 1310744
  2.0 9.7 %multiply_reduce_fusion.6 = (f32[160]{0:T(256)S(1)}, f32[2048]{0:T(1024)S(1)}, f32[160,2048]{1,0:T(8,128)}) fusion(bf16[4096,160]{0,1:T(8,128)(2,1)S(1)} %copy-done, bf16[4096,2048]{1,0:T(8,128)(2,1)} %param.17), kind=kOutput, calls=%fused_computation.22 | convolution fusion | flops 2685335296 | bytes 19407488 | tf_op jit(solution)/shard_map/ti,tj->ij/dot_general | solution.py:87
  11.7 30.7 %multiply_reduce_fusion.1 = (f32[2,5120]{1,0:T(2,128)S(1)}, f32[2,64,5120]{2,1,0:T(8,128)}) fusion(bf16[2,4096,5120]{2,1,0:T(8,128)(2,1)} %param.16, bf16[4096,64]{0,1:T(8,128)(2,1)S(1)} %copy-done.3), kind=kOutput, calls=%fused_computation.3 | convolution fusion | flops 5370009600 | bytes 87072768 | tf_op jit(solution)/shard_map/ti,ktj->kij/dot_general | solution.py:86
  42.5 0.6 reduce_sum.147
  43.1 0.9 multiply_reduce_fusion.5
  44.0 2.2 %multiply_reduce_fusion = f32[2]{0:T(128)S(1)} fusion(f32[2,64,5120]{2,1,0:T(8,128)} %param.18), kind=kLoop, calls=%fused_computation.2 | loop fusion | flops 1310718 | bytes 2621448 | tf_op jit(solution)/shard_map/reduce_sum | solution.py:92
  46.3 1.4 %select_maximum_fusion.2 = f32[128]{0:T(128)S(1)} fusion(f32[1]{0:T(128)} %bitcast.3, f32[2]{0:T(128)S(1)} %multiply_reduce_fusion, f32[1]{0:T(128)} %bitcast.2, f32[2]{0:T(128)S(1)} %reduce_sum.146), kind=kLoop, calls=%fused_computation.42 | loop fusion | flops 1024 | bytes 536 | tf_op jit(solution)/shard_map/concatenate | solution.py:91
  47.7 0.6 pad_maximum_fusion.1.refs_0_
  48.4 17.8 %all_sum.1 = f32[32,4,128]{2,1,0:T(4,128)} custom-call(f32[32,4,128]{2,1,0:T(4,128)} %pad_maximum_fusion.1.refs_0_), custom_call_target="tpu_custom_call" | custom-call | tf_op jit(solution)/shard_map/all_sum/pallas_call | solution.py:46
  66.1 1.5 %slice_reduce_fusion.3 = (f32[]{:T(128)}, f32[32,3,128]{2,1,0:T(4,128)S(1)}) fusion(f32[32,4,128]{2,1,0:T(4,128)} %all_sum.1), kind=kLoop, calls=%fused_computation.58 | loop fusion | flops 12287 | bytes 98308 | tf_op jit(solution)/shard_map/reduce_sum | solution.py:98
  69.7 0.6 fusion.11
  71.0 1.5 %fusion.14 = (f32[1,1,1]{2,1,0:T(1,128)}, f32[1,1,1]{2,1,0:T(1,128)}, f32[1,1,1]{2,1,0:T(1,128)}, f32[1,1,1]{2,1,0:T(1,128)}, f32[1,1,1]{2,1,0:T(1,128)}, /*index=5*/f32[1,1,1]{2,1,0:T(1,128)}) fusion(f32[32,4,128]{2,1,0:T(4,128)} %all_sum.1), kind=kLoop, calls=%fused_computation.62 | loop fusion | bytes 48 | tf_op jit(solution)/shard_map/slice | solution.py:118
  74.5 2.1 %multiply_reduce_fusion.4 = (f32[64]{0:T(128)S(1)}, f32[64]{0:T(128)S(1)}) fusion(f32[2,64,5120]{2,1,0:T(8,128)} %get-tuple-element.48), kind=kLoop, calls=%fused_computation.18 | loop fusion | flops 1310592 | bytes 2621952 | tf_op jit(solution)/shard_map/reduce_sum | solution.py:104
  77.0 1.4 %fusion.5 = (f32[]{:T(128)}, f32[]{:T(128)}) fusion(f32[2,64,5120]{2,1,0:T(8,128)S(1)} %copy-done.1, f32[5120]{0:T(1024)S(1)} %get-tuple-element.32, f32[64]{0:T(128)S(1)} %get-tuple-element.45, f32[]{:T(128)S(6)} %min.3, f32[5120]{0:T(1024)S(1)} %get-tuple-element.14, f32[64]{0:T(128)S(1)} %get-tuple-element.44), kind=kLoop, calls=%fused_computation.11 | loop fusion | flops 3276798 | bytes 2662924 | tf_op jit(solution)/shard_map/reduce_sum | solution.py:108
  78.3 1.2 %fusion.13 = (f32[2048]{0:T(1024)S(1)}, f32[2048]{0:T(1024)}, f32[]{:T(128)}) fusion(f32[12288]{0:T(1024)S(1)} %reshape.172, f32[]{:T(128)S(6)} %mul.368, f32[]{:T(128)S(6)} %sub.14, f32[2048]{0:T(1024)S(1)} %copy-done.6, f32[]{:T(128)S(6)} %copy.21), kind=kLoop, calls=%fused_computation.61 | loop fusion | flops 14335 | bytes 32784 | tf_op jit(solution)/shard_map/rsqrt | solution.py:107
  81.4 2.3 %multiply_reduce_fusion.2 = f32[]{:T(128)} fusion(f32[160,2048]{1,0:T(8,128)} %get-tuple-element.46, f32[2048]{0:T(1024)S(1)} %get-tuple-element.20, f32[160]{0:T(256)S(1)} %get-tuple-element.18, f32[]{:T(128)S(6)} %min.3), kind=kLoop, calls=%fused_computation.15 | loop fusion | flops 1638399 | bytes 1319560 | tf_op jit(solution)/shard_map/reduce_sum | solution.py:108
  83.8 2.1 %select_maximum_fusion = f32[128]{0:T(128)S(1)} fusion(f32[1]{0:T(128)} %bitcast.16, f32[1]{0:T(128)} %bitcast.14, f32[1]{0:T(128)} %bitcast.9), kind=kLoop, calls=%fused_computation.39 | loop fusion | flops 768 | bytes 524 | tf_op jit(solution)/shard_map/stack | solution.py:112
  85.8 0.6 broadcast_in_dim.21.refs_0_
  86.4 8.7 %small_sum.1 = f32[8,128]{1,0:T(8,128)} custom-call(f32[8,128]{1,0:T(8,128)} %broadcast_in_dim.21.refs_0_), custom_call_target="tpu_custom_call" | custom-call | tf_op jit(solution)/shard_map/small_sum/pallas_call | solution.py:71
  95.1 1.4 %fusion.15 = (f32[1,1]{1,0:T(1,128)}, f32[1,1]{1,0:T(1,128)}, f32[1,1]{1,0:T(1,128)}) fusion(f32[8,128]{1,0:T(8,128)} %small_sum.1), kind=kLoop, calls=%fused_computation.63 | loop fusion | bytes 24 | tf_op jit(solution)/shard_map/slice | solution.py:117
  99.1 2.7 %multiply_subtract_fusion = f32[160,2048]{1,0:T(8,128)} fusion(f32[160,2048]{1,0:T(8,128)S(1)} %copy-done.2, f32[160,2048]{1,0:T(8,128)} %get-tuple-element.46, f32[]{:T(128)S(6)} %max.35, f32[]{:T(128)S(6)} %mul.445, f32[2048]{0:T(1024)S(1)} %get-tuple-element.20, f32[160]{0:T(256)S(1)} %get-tuple-element.18, f32[]{:T(128)S(6)} %min.3), kind=kLoop, calls=%fused_computation.12 | loop fusion | flops 1966080 | bytes 3941004 | tf_op jit(solution)/shard_map/sub | solution.py:119
  104.5 3.1 %multiply_subtract_fusion.2 = (f32[1,64,5120]{2,1,0:T(8,128)S(1)}, f32[1,64,5120]{2,1,0:T(8,128)S(1)}) fusion(f32[2,64,5120]{2,1,0:T(8,128)} %param.18, f32[2,64,5120]{2,1,0:T(8,128)} %get-tuple-element.48, f32[]{:T(128)S(6)} %max.29, f32[5120]{0:T(1024)S(1)} %get-tuple-element.32, f32[64]{0:T(128)S(1)} %get-tuple-element.45, f32[]{:T(128)S(6)} %min.3, ...), kind=kLoop, calls=%fused_computation.14 | loop fusion | flops 3932160 | bytes 7905812 | tf_op jit(solution)/shard_map/sub | solution.py:119
  107.6 1.7 %pad_maximum_fusion = f32[2,64,5120]{2,1,0:T(8,128)} fusion(f32[1,64,5120]{2,1,0:T(8,128)S(1)} %get-tuple-element.23, f32[1,64,5120]{2,1,0:T(8,128)S(1)} %get-tuple-element.22), kind=kLoop, calls=%fused_computation.1 | loop fusion | flops 655360 | bytes 5242880 | tf_op jit(solution)/shard_map/stack | solution.py:121
  109.3 0.7 pad_maximum_fusion.3
  (26 shorter events, 1.8 us)
Async XLA Ops:
  0.6 1.3 %copy-start = (bf16[4096,160]{0,1:T(8,128)(2,1)S(1)}, bf16[4096,160]{0,1:T(8,128)(2,1)}, u32[]{:S(2)}) copy-start(bf16[4096,160]{0,1:T(8,128)(2,1)} %param.15) | copy-start | bytes 3932164
  0.6 11.0 %copy-start.3 = (bf16[4096,64]{0,1:T(8,128)(2,1)S(1)}, bf16[4096,64]{0,1:T(8,128)(2,1)}, u32[]{:S(2)}) copy-start(bf16[4096,64]{0,1:T(8,128)(2,1)} %param.14) | copy-start | bytes 1572868
  11.7 30.8 %copy-start.7 = (f32[160]{0:T(256)S(1)}, f32[160]{0:T(256)}, u32[]{:S(2)}) copy-start(f32[160]{0:T(256)} %param.22) | copy-start | bytes 1924
  11.7 31.4 %copy-start.2 = (f32[160,2048]{1,0:T(8,128)S(1)}, f32[160,2048]{1,0:T(8,128)}, u32[]{:S(2)}) copy-start(f32[160,2048]{1,0:T(8,128)} %param.19) | copy-start | bytes 3932164
  44.0 2.2 %copy-start.5 = (f32[2,64]{1,0:T(2,128)S(1)}, f32[2,64]{1,0:T(2,128)}, u32[]{:S(2)}) copy-start(f32[2,64]{1,0:T(2,128)} %param.20) | copy-start | bytes 1540
  44.0 25.6 %copy-start.4 = (f32[2,5120]{1,0:T(2,128)S(1)}, f32[2,5120]{1,0:T(2,128)}, u32[]{:S(2)}) copy-start(f32[2,5120]{1,0:T(2,128)} %param.21) | copy-start | bytes 122884
  74.4 2.5 %copy-start.1 = (f32[2,64,5120]{2,1,0:T(8,128)S(1)}, f32[2,64,5120]{2,1,0:T(8,128)}, u32[]{:S(2)}) copy-start(f32[2,64,5120]{2,1,0:T(8,128)} %get-tuple-element.48) | copy-start | bytes 7864324
  77.0 1.4 %copy-start.6 = (f32[2048]{0:T(1024)S(1)}, f32[2048]{0:T(1024)}, u32[]{:S(2)}) copy-start(f32[2048]{0:T(1024)} %param.23) | copy-start | bytes 24580

commit v2 on v0

v2 whole, which is shorter than its diff:
```python
import jax
import jax.numpy as jnp
from jax import lax
from jax.experimental import pallas as pl
from jax.experimental.pallas import tpu as pltpu
from jax.sharding import PartitionSpec as P

EPS_ONE = 1e-30
EPS_TWO = 1e-3
LANES = 128
STRIPE = 512
BLOCKS = STRIPE // LANES
EARLY = 8
LATE = 4
F32 = jnp.float32
MESH = pl.DeviceIdType.MESH


def grads_kernel(n, x_hbm, h_hbm, dyi_hbm, dyo_hbm, wi_hbm, wo_hbm, ri_hbm, ci_hbm, ro_hbm, co_hbm,
                 beta_hbm, step_hbm, rms_hbm, norm_hbm,
                 gi, go, wi, wo, ri_new, ci_new, ro_new, co_new, coef,
                 xs, hs, dy, si, so, csend, rs_land, ag_send, ag_land, late_land, csum, colf, ai, ao,
                 fsend, f_land, ri, ci, ro, co, beta, step, rms, norm,
                 dy_sem, x_sem, w_sem, small_sem, xs_sem, g_sem, rs_sem, ag_sem, late_sem, f_sem):
    me = lax.axis_index('tp')
    core = lax.rem(me, 2)
    chip = me // 2
    x, y, z = lax.rem(chip, 2), lax.rem(chip // 2, 2), chip // 4
    partner = me + 1 - 2 * core
    peers = []
    for dz in (2, 1, 3, 0):
        for dy_ in (1, 0):
            for dx in (1, 0):
                for dc in (0, 1):
                    if dz or dy_ or dx or dc:
                        peers.append(((lax.rem(z + dz, n // 8) * 2 + lax.rem(y + dy_, 2)) * 2 + lax.rem(x + dx, 2)) * 2
                                     + lax.rem(core + dc, 2))
    kinds, m_in, cols_in = wi.shape
    m_out, cols_out = wo.shape
    half_in, half_out = cols_in // 2, cols_out // 2
    per_in, per_out = half_in // STRIPE, half_out // STRIPE
    n_in = kinds * per_in
    slots = dy.shape[0]

    def remote(src, dst, sems, peer):
        return pltpu.make_async_remote_copy(src_ref=src, dst_ref=dst, send_sem=sems.at[0], recv_sem=sems.at[1],
                                            device_id=(peer,), device_id_type=MESH)

    def to_all(src, dst, sems):
        for peer in peers:
            remote(src, dst, sems, peer).start()

    def wait_for(ref, sem):
        pltpu.make_async_copy(ref, ref, sem).wait()

    def out_copy(s):
        cols = pl.ds(pl.multiple_of(core * half_out + s * STRIPE, LANES), STRIPE)
        return pltpu.make_async_copy(dyo_hbm.at[:, cols], dy.at[s], dy_sem.at[s])

    def in_copy(t):
        slot = lax.rem(t + per_out, slots)
        cols = pl.ds(pl.multiple_of(core * half_in + lax.rem(t, per_in) * STRIPE, LANES), STRIPE)
        return pltpu.make_async_copy(dyi_hbm.at[t // per_in, :, cols], dy.at[slot], dy_sem.at[slot])

    barrier = pltpu.get_barrier_semaphore()
    x_copy = pltpu.make_async_copy(x_hbm, xs.at[pl.ds(0, m_in)], x_sem.at[0])
    h_copy = pltpu.make_async_copy(h_hbm, hs.at[pl.ds(0, m_out)], x_sem.at[1])
    x_copy.start()
    h_copy.start()
    for peer in peers:
        pl.semaphore_signal(barrier, inc=1, device_id=(peer,), device_id_type=MESH)
    for s in range(per_out):
        out_copy(s).start()
    small = [pltpu.make_async_copy(src, dst, small_sem.at[i]) for i, (src, dst) in enumerate(
        ((ri_hbm, ri), (ci_hbm, ci), (ro_hbm, ro), (co_hbm, co), (beta_hbm, beta), (step_hbm, step), (rms_hbm, rms), (norm_hbm, norm)))]
    for copy in small:
        copy.start()
    for t in range(slots - per_out):
        in_copy(t).start()
    x_copy.wait()
    h_copy.wait()
    pl.semaphore_wait(barrier, n - 1)
    x_send = remote(xs.at[pl.ds(0, m_in)], xs.at[pl.ds(m_in, m_in)], xs_sem.at[0], partner)
    h_send = remote(hs.at[pl.ds(0, m_out)], hs.at[pl.ds(m_out, m_out)], xs_sem.at[1], partner)
    x_send.start()
    h_send.start()

    def put_cols(index, col_sq, add):
        for r in range(BLOCKS):
            part = col_sq[:, r * LANES:(r + 1) * LANES]
            where = (index + r // 2, pl.ds(r % 2, 1), slice(None))
            csend[where] = csend[where] + part if add else part

    def to_owner(p):
        for h in range(2):
            owner = 2 * p + h

            @pl.when(chip != owner)
            def _():
                remote(csend.at[owner], rs_land.at[chip], rs_sem, 2 * owner + core).start()

            @pl.when(chip == owner)
            def _():
                rs_land[chip] = csend[owner]

    for s in range(per_out):
        out_copy(s).wait()
        own = jnp.dot(hs[0:m_out, :], dy[s], preferred_element_type=F32)
        go[s, core] = own
        put_cols(2 * s, jnp.sum(own * own, axis=0, keepdims=True), False)
    for copy in small:
        copy.wait()
    lane = lax.broadcasted_iota(jnp.int32, (1, LANES), 1)

    def pack(values):
        row = jnp.zeros((1, LANES), F32)
        for i, value in enumerate(values):
            row = jnp.where(lane == i, value, row)
        return row

    ag_send[3:4, :] = jnp.zeros((1, LANES), F32)
    ag_send[2:3, :] = pack([jnp.sum(ri[k:k + 1, :], axis=1, keepdims=True) for k in range(kinds)]
                           + [jnp.sum(ro[...], axis=1, keepdims=True)])
    x_send.wait_recv()
    h_send.wait_recv()
    for s in range(per_out):
        other = jnp.dot(hs[m_out:2 * m_out, :], dy[s], preferred_element_type=F32)
        so[s] = other
        remote(so.at[s], go.at[s, core], g_sem.at[0], partner).start()
        put_cols(2 * s, jnp.sum(other * other, axis=0, keepdims=True), True)
        to_owner(s)
    for t in range(slots - per_out, n_in):
        in_copy(t).start()

    def in_step(t, carry):
        in_copy(t).wait()
        p = t + per_out
        both = jnp.dot(xs[...], dy[lax.rem(p, slots)], preferred_element_type=F32)
        gi[t, core] = both[0:m_in]
        si[t] = both[m_in:2 * m_in]
        remote(si.at[t], gi.at[t, core], g_sem.at[1], partner).start()
        put_cols(2 * p, jnp.sum(both * both, axis=0, keepdims=True), False)

        @pl.when(p < EARLY)
        def _():
            to_owner(p)

        @pl.when(p >= EARLY)
        def _():
            to_all(csend.at[pl.ds(2 * p, 2)], late_land.at[p - EARLY, me], late_sem)
            late_land[p - EARLY, me] = csend[pl.ds(2 * p, 2)]

        @pl.when(t == n_in - 2)
        def _():
            wait_for(rs_land.at[pl.ds(0, n // 2 - 1)], rs_sem.at[1])
            ag_send[0:2, :] = jnp.sum(rs_land[...], axis=0)
            to_all(ag_send, ag_land.at[me], ag_sem)
            ag_land[me] = ag_send[...]

        return carry

    lax.fori_loop(0, n_in, in_step, 0)
    wi_copy = pltpu.make_async_copy(wi_hbm, wi, w_sem.at[0])
    wo_copy = pltpu.make_async_copy(wo_hbm, wo, w_sem.at[1])
    wi_copy.start()
    wo_copy.start()

    wait_for(so, g_sem.at[0, 1])
    wait_for(si, g_sem.at[1, 1])

    def row_sq(ref, blocks):
        rows = ref.shape[2]

        def add(t, total):
            for c in range(2):
                for r in range(BLOCKS):
                    g = ref[t, c, :, r * LANES:(r + 1) * LANES]
                    total = total + g * g
            return total

        return jnp.sum(lax.fori_loop(blocks[0], blocks[1], add, jnp.zeros((rows, LANES), F32)), axis=1, keepdims=True)

    row_sums = [row_sq(gi, (k * per_in, (k + 1) * per_in)) for k in range(kinds)] + [row_sq(go, (0, per_out))]
    wi_copy.wait()
    wo_copy.wait()
    w_sums = [jnp.sum(wi[k] * wi[k], axis=(0, 1), keepdims=True) for k in range(kinds)]
    w_sums.append(jnp.sum(wo[...] * wo[...], axis=(0, 1), keepdims=True))

    wait_for(ag_land.at[pl.ds(0, n - 1)], ag_sem.at[1])
    wait_for(late_land.at[:, pl.ds(0, n - 1)], late_sem.at[1])
    for c in range(2):
        for q in range(2 * EARLY):
            csum[c, q] = ag_land[2 * q + c, 0:2, :]
        for stripe in range(LATE):
            total = late_land[stripe, c]
            for q in range(1, n // 2):
                total = total + late_land[stripe, 2 * q + c]
            csum[c, pl.ds(2 * (EARLY + stripe), 2)] = total
    misc = ag_land[0, 2:3, :]
    for d in range(1, n):
        misc = misc + ag_land[d, 2:3, :]

    def at_lane(row, i):
        return jnp.sum(jnp.where(lane == i, row, 0.0), axis=1, keepdims=True)

    first = [2 * (per_out + k * per_in) for k in range(kinds)] + [0]
    count = [2 * per_in] * kinds + [2 * per_out]
    rows_of = [m_in * n] * kinds + [m_out * n]
    cols_of = [cols_in] * kinds + [cols_out]
    grand = []
    for i in range(kinds + 1):
        part = jnp.sum(csum[:, first[i]:first[i] + count[i]], axis=(0, 1))
        grand.append(jnp.sum(part, axis=(0, 1), keepdims=True))
    norm_sq = grand[0]
    for g in grand[1:]:
        norm_sq = norm_sq + g
    scale = jnp.minimum(1.0, norm[...] / jnp.sqrt(norm_sq))
    keep = beta[...]
    mix = 1.0 - keep

    for i in range(kinds + 1):
        rows = m_out if i == kinds else m_in
        level = keep * (at_lane(misc, i) / rows_of[i]) + mix * (scale * (scale * (grand[i] / (rows_of[i] * cols_of[i]))) + EPS_ONE)
        eye = lax.broadcasted_iota(jnp.int32, (rows, rows), 0) == lax.broadcasted_iota(jnp.int32, (rows, rows), 1)
        old = ro[...] if i == kinds else ri[i:i + 1, :]
        old = jnp.sum(jnp.where(eye, old, 0.0), axis=1, keepdims=True)
        new = keep * old + mix * (scale * (scale * (row_sums[i] / cols_of[i])) + EPS_ONE)
        factor = jnp.broadcast_to(scale * lax.rsqrt(new / level), (rows, LANES))
        flat = jnp.sum(jnp.where(eye, new, 0.0), axis=0, keepdims=True)
        if i == kinds:
            ao[...] = factor
            ro_new[...] = flat
        else:
            ai[i] = factor
            ri_new[i:i + 1, :] = flat

    for c in range(2):
        for p in range(per_out + n_in):
            for r in range(BLOCKS):
                where = (c, 2 * p + r // 2, pl.ds(r % 2, 1), slice(None))
                if p < per_out:
                    i = kinds
                    spot = (pl.ds((c * half_out + p * STRIPE) // LANES + r, 1), slice(None))
                    old, store = co, co_new
                else:
                    i, s = divmod(p - per_out, per_in)
                    spot = (pl.ds(i, 1), pl.ds(c * half_in + s * STRIPE + r * LANES, LANES))
                    old, store = ci, ci_new
                new = keep * old[spot] + mix * (scale * (scale * (csum[where] / rows_of[i])) + EPS_ONE)
                store[spot] = new
                colf[where] = lax.rsqrt(new)

    def update(ref, factor, p0, blocks):
        def step_(t, total):
            for c in range(2):
                for r in range(BLOCKS):
                    col = colf[c, 2 * (p0 + t) + r // 2, pl.ds(r % 2, 1), :]
                    u = ref[t, c, :, r * LANES:(r + 1) * LANES] * factor * col
                    ref[t, c, :, r * LANES:(r + 1) * LANES] = u
                    total = total + u * u
            return total

        total = lax.fori_loop(blocks[0], blocks[1], step_, jnp.zeros(factor.shape, F32))
        return jnp.sum(total, axis=(0, 1), keepdims=True)

    u_sums = [update(gi, ai[k], per_out, (k * per_in, (k + 1) * per_in)) for k in range(kinds)]
    u_sums.append(update(go, ao[...], 0, (0, per_out)))
    fsend[...] = pack(u_sums + w_sums)
    to_all(fsend, f_land.at[me], f_sem)
    f_land[me] = fsend[...]
    wait_for(f_land.at[pl.ds(0, n - 1)], f_sem.at[1])
    sums = f_land[0]
    for d in range(1, n):
        sums = sums + f_land[d]
    for i in range(kinds + 1):
        size = float(rows_of[i] * cols_of[i])
        clip = jnp.maximum(1.0, jnp.sqrt(at_lane(sums, i) / size) / rms[...])
        move = step[...] * jnp.maximum(EPS_TWO, jnp.sqrt(at_lane(sums, kinds + 1 + i) / size))
        coef[i:i + 1, :] = jnp.broadcast_to(move / clip, (1, LANES))

    x_send.wait_send()
    h_send.wait_send()
    wait_for(so, g_sem.at[0, 0])
    wait_for(si, g_sem.at[1, 0])
    wait_for(rs_land.at[pl.ds(0, n // 2 - 1)], rs_sem.at[0])
    wait_for(ag_land.at[pl.ds(0, n - 1)], ag_sem.at[0])
    wait_for(late_land.at[:, pl.ds(0, n - 1)], late_sem.at[0])
    wait_for(f_land.at[pl.ds(0, n - 1)], f_sem.at[0])


def apply_kernel(gi, go, wi, wo, ri, ci, ro, co, coef, wi_out, ri_out, ci_out, wo_out, ro_out, co_out, wi_new, wo_new, sems):
    kinds, m_in, cols_in = wi.shape
    per_in, per_out = gi.shape[0] // kinds, go.shape[0]
    copies = []

    def send(src, dst):
        copies.append(pltpu.make_async_copy(src, dst, sems.at[len(copies)]))
        copies[-1].start()

    send(ri, ri_out)
    send(ci, ci_out)
    send(ro, ro_out)
    send(co, co_out)
    for k in range(kinds):
        for c in range(2):
            for s in range(per_in):
                cols = pl.ds(c * (cols_in // 2) + s * STRIPE, STRIPE)
                wi_new[k, :, cols] = wi[k, :, cols] - coef[k:k + 1, 0:1] * gi[k * per_in + s, c]
            part = pl.ds(c * (cols_in // 2), cols_in // 2)
            send(wi_new.at[k, :, part], wi_out.at[k, :, part])
    half = wo.shape[1] // 2
    for c in range(2):
        for s in range(per_out):
            cols = pl.ds(c * half + s * STRIPE, STRIPE)
            wo_new[:, cols] = wo[:, cols] - coef[kinds:kinds + 1, 0:1] * go[s, c]
        part = pl.ds(c * half, half)
        send(wo_new.at[:, part], wo_out.at[:, part])
    for copy in copies:
        copy.wait()


def solution(mesh):
    n = mesh.shape['tp']

    def local_step(x_norm, hid_act, dy_in, dy_out, w_in, w_out, row_in, col_in, row_out, col_out, beta_two, rel_step, clip_rms, clip_norm):
        kinds, m_in, cols_in = w_in.shape
        m_out, cols_out = w_out.shape
        tokens = x_norm.shape[0]
        n_in, n_out = kinds * cols_in // (2 * STRIPE), cols_out // (2 * STRIPE)
        stripes = n_in + n_out
        assert stripes == EARLY + LATE and n == 2 * 2 * EARLY
        slots = 10
        ins = [x_norm.T, hid_act.T, dy_in, dy_out, w_in, w_out, row_in, col_in, row_out.reshape(1, -1), col_out.reshape(-1, LANES)]
        ins += [v.reshape(1, 1) for v in (beta_two, rel_step, clip_rms, clip_norm)]
        outs = [(n_in, 2, m_in, STRIPE), (n_out, 2, m_out, STRIPE), w_in.shape, w_out.shape, row_in.shape, col_in.shape,
                (1, m_out), (cols_out // LANES, LANES), (8, LANES)]
        vmem = [((2 * m_in, tokens), jnp.bfloat16), ((2 * m_out, tokens), jnp.bfloat16), ((slots, tokens, STRIPE), jnp.bfloat16),
                ((n_in, m_in, STRIPE), F32), ((n_out, m_out, STRIPE), F32), ((2 * stripes, 2, LANES), F32),
                ((n // 2, 2, LANES), F32), ((4, LANES), F32), ((n, 4, LANES), F32), ((LATE, n, 2, 2, LANES), F32),
                ((2, 2 * stripes, 2, LANES), F32), ((2, 2 * stripes, 2, LANES), F32),
                ((kinds, m_in, LANES), F32), ((m_out, LANES), F32), ((1, LANES), F32), ((n, 1, LANES), F32),
                (row_in.shape, F32), (col_in.shape, F32), ((1, m_out), F32), ((cols_out // LANES, LANES), F32)]
        vmem += [((1, 1), F32)] * 4
        sems = [(slots,), (2,), (2,), (8,), (2, 2), (2, 2), (2,), (2,), (2,), (2,)]
        anywhere = pl.BlockSpec(memory_space=pl.ANY)
        inside = pl.BlockSpec(memory_space=pltpu.VMEM)
        mid = pl.pallas_call(
            lambda *refs: grads_kernel(n, *refs),
            out_shape=[pltpu.VMEM(s, F32) for s in outs],
            in_specs=[anywhere] * len(ins),
            out_specs=[inside] * len(outs),
            scratch_shapes=[pltpu.VMEM(*v) for v in vmem] + [pltpu.SemaphoreType.DMA(s) for s in sems],
            compiler_params=pltpu.CompilerParams(collective_id=0, has_side_effects=True, vmem_limit_bytes=56 * 2**20),
            name='grads',
        )(*ins)
        finals = [w_in.shape, row_in.shape, col_in.shape, w_out.shape, (1, m_out), (cols_out // LANES, LANES)]
        new = pl.pallas_call(
            apply_kernel,
            out_shape=[jax.ShapeDtypeStruct(s, F32) for s in finals],
            in_specs=[inside] * len(mid),
            out_specs=[anywhere] * len(finals),
            scratch_shapes=[pltpu.VMEM(w_in.shape, F32), pltpu.VMEM(w_out.shape, F32), pltpu.SemaphoreType.DMA((10,))],
            compiler_params=pltpu.CompilerParams(vmem_limit_bytes=8 * 2**20),
            name='apply',
        )(*mid)
        return (new[0], new[1], new[2], new[3], new[4].reshape(m_out), new[5].reshape(cols_out))

    in_specs = (P(None, 'tp'), P(None, 'tp'), P(), P(), P(None, 'tp', None), P('tp', None),
                P(None, 'tp'), P(), P('tp'), P(), P(), P(), P(), P())
    out_specs = (P(None, 'tp', None), P(None, 'tp'), P(), P('tp', None), P('tp'), P())
    return jax.shard_map(local_step, mesh=mesh, in_specs=in_specs, out_specs=out_specs, check_vma=False)
```

time: 152 us -> 39.6 us (0.26)
  blocking collectives: 83 us -> 0 us
  matrix products: 38 us -> 0 us
  Pallas kernels: 0 us -> 36.2 us
  other arithmetic: 20.1 us -> 0 us
  between operations: 7.47 us -> 3.23 us
  local copies, waits for them, and re-layouts: 2.41 us -> 0 us
    psum x2 -> x0, blocking collectives: 83 us -> none  [the longest x1 42.6 us: local_step(): totals_in = lax.psum(local_sums(grad_in, w_in, row_in), 'tp')]
    dot_general x2 -> x0, matrix products: 38 us -> none  [the longest x1 30.6 us: local_step(): jnp.einsum('ti,ktj->kij', x_norm, dy_in, preferred_element_type=jnp.float32)]
    pallas_call x0 -> x2, Pallas kernels: none -> 36.2 us  [the longest x1 33.8 us: local_step(): pl.pallas_call(lambda *refs: grads_kernel(n, *refs), out_shape=[pltpu.VME...]
    reduce_sum x10 -> x0, other arithmetic: 11.8 us -> none  [the longest x2 4.43 us: local_sums(): w_sq = jnp.sum(weight * weight, axis=(-2, -1))[..., None]]
    sub x2 -> x0, other arithmetic: 6.9 us -> none  [apply_update(): return (weight - step_size * clipped, row_new, col_new)]
where the time goes in v2:
time: 39.6 us; the launch traced here: 39.4 us
  Pallas kernels  36.2 us (91%)
  between operations  3.23 us (8%)
    pallas_call x1, Pallas kernels, local_step(): pl.pallas_call(lambda *refs: grads_kernel(n, *refs), out_shape=[pltpu.VME...  33.8 us
    pallas_call x1, Pallas kernels, local_step(): pl.pallas_call(apply_kernel, out_shape=[jax.ShapeDtypeStruct(s, F32) for...  2.34 us

profile of v2, /device:TPU:0, one launch (start us, length us, event | category | flops | bytes accessed | tf_op | source)
XLA Modules:
  0.0 39.4 jit_solution(667205903202665016)
XLA Ops:
  3.2 33.8 %grads.1 = (f32[10,2,64,512]{3,2,1,0:T(8,128)S(1)}, f32[2,2,160,512]{3,2,1,0:T(8,128)S(1)}, f32[2,64,5120]{2,1,0:T(8,128)S(1)}, f32[160,2048]{1,0:T(8,128)S(1)},...) custom-call(bf16[64,4096]{1,0:T(8,128)(2,1)} %bitcast.15, ...), custom_call_target="tpu_custom_call" | custom-call | tf_op jit(solution)/shard_map/grads/pallas_call | solution.py:347
  37.0 2.3 %apply.1 = (f32[2,64,5120]{2,1,0:T(8,128)}, f32[2,64]{1,0:T(2,128)}, f32[2,5120]{1,0:T(2,128)}, f32[160,2048]{1,0:T(8,128)}, f32[1,160]{1,0:T(1,128)}, /*index=5*/f32[16,128]{1,0:T(8,128)}) custom-call(f32[10,2,64,512]{3,2,1,0:T(8,128)S(1)} %get-tuple-element.21.gi, f32[2,2,160,512]{3,2,1,0:T(8,128)S(1)} %get-tuple-element.22.go, ...), custom_call_target="tpu_custom_call" | custom-call | tf_op jit(solution)/shard_map/apply/pallas_call | solution.py:357

commit v3 on v2

v3 whole, which is shorter than its diff:
```python
import jax
import jax.numpy as jnp
from jax import lax
from jax.experimental import pallas as pl
from jax.experimental.pallas import tpu as pltpu
from jax.sharding import PartitionSpec as P

EPS_ONE = 1e-30
EPS_TWO = 1e-3
LANES = 128
STRIPE = 512
HALF = STRIPE // 2
LAST = 2
F32 = jnp.float32
MESH = pl.DeviceIdType.MESH


def grads_kernel(n, x_hbm, h_hbm, dyi_hbm, dyo_hbm, wi_hbm, wo_hbm, ri_hbm, ci_hbm, ro_hbm, co_hbm,
                 scal_hbm,
                 gi, go, wi, wo, ri_new, ci_new, ro_new, co_new, coef, ai, ao, colf,
                 xs, hs, dy, si, so, csend, land, misc_land, last_land, csum,
                 fsend, f_land, ri, ci, ro, co, scal,
                 dy_sem, x_sem, w_sem, small_sem, xs_sem, g_sem, land_sem, misc_sem, last_sem, fwd_sem, f_sem):
    me = lax.axis_index('tp')
    core = lax.rem(me, 2)
    chip = me // 2
    x, y, z = lax.rem(chip, 2), lax.rem(chip // 2, 2), chip // 4
    partner = me + 1 - 2 * core
    peers = {0: [], 1: []}
    for dz in (2, 1, 3, 0):
        for dy_ in (1, 0):
            for dx in (1, 0):
                for dc in (0, 1):
                    if dz or dy_ or dx or dc:
                        peers[dc].append(((lax.rem(z + dz, n // 8) * 2 + lax.rem(y + dy_, 2)) * 2 + lax.rem(x + dx, 2)) * 2
                                         + lax.rem(core + dc, 2))
    same = peers[0]
    everyone = [p for pair in zip(peers[0] + [None], peers[1]) for p in pair if p is not None]
    kinds, m_in, cols_in = wi.shape
    m_out, cols_out = wo.shape
    half_in, half_out = cols_in // 2, cols_out // 2
    per_in, per_out = half_in // STRIPE, half_out // STRIPE
    n_in = kinds * per_in
    stripes = n_in + per_out
    slots = dy.shape[0]
    early = land.shape[0]

    def remote(src, dst, sems, peer):
        return pltpu.make_async_remote_copy(src_ref=src, dst_ref=dst, send_sem=sems.at[0], recv_sem=sems.at[1],
                                            device_id=(peer,), device_id_type=MESH)

    def to_all(src, dst, sems, who):
        for peer in who:
            remote(src, dst, sems, peer).start()

    def wait_for(ref, sem):
        pltpu.make_async_copy(ref, ref, sem).wait()

    def out_copy(s):
        cols = pl.ds(pl.multiple_of(core * half_out + s * STRIPE, LANES), STRIPE)
        return pltpu.make_async_copy(dyo_hbm.at[:, cols], dy.at[s], dy_sem.at[s])

    def in_copy(t):
        slot = lax.rem(t + per_out, slots)
        cols = pl.ds(pl.multiple_of(core * half_in + lax.rem(t, per_in) * STRIPE, LANES), STRIPE)
        return pltpu.make_async_copy(dyi_hbm.at[t // per_in, :, cols], dy.at[slot], dy_sem.at[slot])

    barrier = pltpu.get_barrier_semaphore()
    x_copy = pltpu.make_async_copy(x_hbm, xs.at[pl.ds(0, m_in)], x_sem.at[0])
    h_copy = pltpu.make_async_copy(h_hbm, hs.at[pl.ds(0, m_out)], x_sem.at[1])
    x_copy.start()
    h_copy.start()
    out_copy(0).start()
    for peer in everyone:
        pl.semaphore_signal(barrier, inc=1, device_id=(peer,), device_id_type=MESH)
    for s in range(1, per_out):
        out_copy(s).start()
    small = [pltpu.make_async_copy(src, dst, small_sem.at[i]) for i, (src, dst) in enumerate(
        ((ri_hbm, ri), (ci_hbm, ci), (ro_hbm, ro), (co_hbm, co), (scal_hbm, scal)))]
    for copy in small:
        copy.start()

    def put_cols(p, h, col_sq, add):
        for r in range(2):
            part = col_sq[:, r * LANES:(r + 1) * LANES]
            where = (1 + 2 * p + h, pl.ds(r, 1), slice(None))
            csend[where] = csend[where] + part if add else part

    def share(p):
        mine = csend.at[pl.ds(1 + 2 * p, 2)]
        to_all(mine, land.at[p, chip], land_sem, same)
        land[p, chip] = mine[...]

    x_copy.wait()
    h_copy.wait()
    in_copy(0).start()
    in_copy(1).start()
    pl.semaphore_wait(barrier, n - 1)
    h_send = remote(hs.at[pl.ds(0, m_out)], hs.at[pl.ds(m_out, m_out)], xs_sem.at[1], partner)
    x_send = remote(xs.at[pl.ds(0, m_in)], xs.at[pl.ds(m_in, m_in)], xs_sem.at[0], partner)
    h_send.start()
    x_send.start()

    for s in range(per_out):
        out_copy(s).wait()
        in_copy(s + 2).start()
        for h in range(2):
            cols = pl.ds(h * HALF, HALF)
            own = jnp.dot(hs[0:m_out, :], dy[s, :, cols], preferred_element_type=F32)
            go[s, core, :, cols] = own
            put_cols(s, h, jnp.sum(own * own, axis=0, keepdims=True), False)
    in_copy(4).start()
    for copy in small:
        copy.wait()
    lane = lax.broadcasted_iota(jnp.int32, (1, LANES), 1)

    def pack(values):
        row = jnp.zeros((1, LANES), F32)
        for i, value in enumerate(values):
            row = jnp.where(lane == i, value, row)
        return row

    csend[0, 1:2, :] = jnp.zeros((1, LANES), F32)
    csend[0, 0:1, :] = pack([jnp.sum(ri[k:k + 1, :], axis=1, keepdims=True) for k in range(kinds)]
                            + [jnp.sum(ro[...], axis=1, keepdims=True)]) + scal[0:1, :]
    to_all(csend.at[0], misc_land.at[chip], misc_sem, same)
    misc_land[chip] = csend[0]
    h_send.wait_recv()
    in_copy(5).start()
    ahead = 6
    for s in range(per_out):
        for h in range(2):
            cols = pl.ds(h * HALF, HALF)
            other = jnp.dot(hs[m_out:2 * m_out, :], dy[s, :, cols], preferred_element_type=F32)
            so[s, :, cols] = other
            put_cols(s, h, jnp.sum(other * other, axis=0, keepdims=True), True)
        remote(so.at[s], go.at[s, core], g_sem.at[0], partner).start()
        share(s)
    x_send.wait_recv()

    def in_step(t, carry):
        in_copy(t).wait()

        @pl.when(t + ahead < n_in)
        def _():
            in_copy(t + ahead).start()

        p = t + per_out
        slot = lax.rem(p, slots)
        for h in range(2):
            cols = pl.ds(h * HALF, HALF)
            both = jnp.dot(xs[...], dy[slot, :, cols], preferred_element_type=F32)
            gi[t, core, :, cols] = both[0:m_in]
            si[t, :, cols] = both[m_in:2 * m_in]
            put_cols(p, h, jnp.sum(both * both, axis=0, keepdims=True), False)

        @pl.when(p < early)
        def _():
            share(p)

        @pl.when(p >= early)
        def _():
            mine = csend.at[pl.ds(1 + 2 * p, 2)]
            to_all(mine, last_land.at[p - early, me], last_sem, everyone)
            last_land[p - early, me] = mine[...]

        remote(si.at[t], gi.at[t, core], g_sem.at[1], partner).start()
        return carry

    lax.fori_loop(0, n_in, in_step, 0)
    wi_copy = pltpu.make_async_copy(wi_hbm, wi, w_sem.at[0])
    wo_copy = pltpu.make_async_copy(wo_hbm, wo, w_sem.at[1])
    wi_copy.start()
    wo_copy.start()

    wait_for(so, g_sem.at[0, 1])
    wait_for(si, g_sem.at[1, 1])

    def row_sq(ref, blocks):
        rows = ref.shape[2]

        def add(t, total):
            for c in range(2):
                for r in range(STRIPE // LANES):
                    g = ref[t, c, :, r * LANES:(r + 1) * LANES]
                    total = total + g * g
            return total

        return jnp.sum(lax.fori_loop(blocks[0], blocks[1], add, jnp.zeros((rows, LANES), F32)), axis=1, keepdims=True)

    row_sums = [row_sq(gi, (k * per_in, (k + 1) * per_in)) for k in range(kinds)] + [row_sq(go, (0, per_out))]

    wait_for(misc_land.at[pl.ds(0, n // 2 - 1)], misc_sem.at[1])
    wait_for(land.at[:, pl.ds(0, n // 2 - 1)], land_sem.at[1])
    csum[core, 0] = jnp.sum(misc_land[...], axis=0)
    for p in range(early):
        csum[core, pl.ds(1 + 2 * p, 2)] = jnp.sum(land[p], axis=0)
    done = csum.at[core, pl.ds(0, 1 + 2 * early)]
    forward = remote(done, done, fwd_sem, partner)
    forward.start()
    wi_copy.wait()
    wo_copy.wait()
    w_sums = [jnp.sum(jnp.sum(wi[k] * wi[k], axis=0, keepdims=True), axis=1, keepdims=True) for k in range(kinds)]
    w_sums.append(jnp.sum(jnp.sum(wo[...] * wo[...], axis=0, keepdims=True), axis=1, keepdims=True))
    forward.wait_recv()
    first = [1 + 2 * (per_out + k * per_in) for k in range(kinds)] + [1]
    count = [2 * per_in] * kinds + [2 * per_out]
    rows_of = [m_in * n] * kinds + [m_out * n]
    cols_of = [cols_in] * kinds + [cols_out]

    def at_lane(row, i):
        return jnp.sum(jnp.where(lane == i, row, 0.0), axis=1, keepdims=True)

    misc = csum[0, 0, 0:1, :] + csum[1, 0, 0:1, :]
    keep, norm, step, rms = (at_lane(misc, kinds + 1 + i) for i in range(4))
    mix = 1.0 - keep
    eyes, olds, levels, grand = [], [], [], []
    for i in range(kinds + 1):
        rows = m_out if i == kinds else m_in
        eyes.append(lax.broadcasted_iota(jnp.int32, (rows, rows), 0) == lax.broadcasted_iota(jnp.int32, (rows, rows), 1))
        old = ro[...] if i == kinds else ri[i:i + 1, :]
        olds.append(keep * jnp.sum(jnp.where(eyes[i], old, 0.0), axis=1, keepdims=True))
        levels.append(keep * (at_lane(misc, i) / rows_of[i]))
        known = min(first[i] + count[i], 1 + 2 * early)
        grand.append(jnp.sum(csum[:, first[i]:known], axis=(0, 1)))
    wait_for(last_land.at[:, pl.ds(0, n - 1)], last_sem.at[1])
    for stripe in range(stripes - early):
        for c in range(2):
            total = last_land[stripe, c]
            for q in range(1, n // 2):
                total = total + last_land[stripe, 2 * q + c]
            csum[c, pl.ds(1 + 2 * (early + stripe), 2)] = total
            grand[kinds - 1] = grand[kinds - 1] + jnp.sum(total, axis=0)
    grand = [jnp.sum(jnp.sum(g, axis=0, keepdims=True), axis=1, keepdims=True) for g in grand]
    norm_sq = grand[0]
    for g in grand[1:]:
        norm_sq = norm_sq + g
    scale = jnp.minimum(1.0, norm / jnp.sqrt(norm_sq))

    for i in range(kinds + 1):
        rows = m_out if i == kinds else m_in
        level = levels[i] + mix * (scale * (scale * (grand[i] / (rows_of[i] * cols_of[i]))) + EPS_ONE)
        new = olds[i] + mix * (scale * (scale * (row_sums[i] / cols_of[i])) + EPS_ONE)
        factor = jnp.broadcast_to(scale * lax.rsqrt(new / level), (rows, LANES))
        if i == kinds:
            ao[...] = factor
        else:
            ai[i] = factor
        olds[i] = new

    for c in range(2):
        for p in range(stripes):
            for r in range(STRIPE // LANES):
                where = (c, 1 + 2 * p + r // 2, pl.ds(r % 2, 1), slice(None))
                if p < per_out:
                    i = kinds
                    spot = (pl.ds((c * half_out + p * STRIPE) // LANES + r, 1), slice(None))
                    old, store = co, co_new
                else:
                    i, s = divmod(p - per_out, per_in)
                    spot = (pl.ds(i, 1), pl.ds(c * half_in + s * STRIPE + r * LANES, LANES))
                    old, store = ci, ci_new
                new = keep * old[spot] + mix * (scale * (scale * (csum[where] / rows_of[i])) + EPS_ONE)
                store[spot] = new
                colf[c, STRIPE // LANES * p + r] = lax.rsqrt(new)

    def update_sq(ref, factor, p0, blocks):
        rows = ref.shape[2]

        def add(t, total):
            for c in range(2):
                for r in range(STRIPE // LANES):
                    part = ref[t, c, :, r * LANES:(r + 1) * LANES] * factor
                    part = part * part
                    fold = part[0:8]
                    for b in range(1, rows // 8):
                        fold = fold + part[8 * b:8 * (b + 1)]
                    col = colf[c, STRIPE // LANES * (p0 + t) + r]
                    total = total + fold * (col * col)
            return total

        total = lax.fori_loop(blocks[0], blocks[1], add, jnp.zeros((8, LANES), F32))
        return jnp.sum(jnp.sum(total, axis=0, keepdims=True), axis=1, keepdims=True)

    u_sums = [update_sq(gi, ai[k], per_out, (k * per_in, (k + 1) * per_in)) for k in range(kinds)]
    u_sums.append(update_sq(go, ao[...], 0, (0, per_out)))
    fsend[...] = pack(u_sums + w_sums)
    to_all(fsend, f_land.at[me], f_sem, everyone)
    f_land[me] = fsend[...]

    for i in range(kinds + 1):
        flat = jnp.sum(jnp.where(eyes[i], olds[i], 0.0), axis=0, keepdims=True)
        if i == kinds:
            ro_new[...] = flat
        else:
            ri_new[i:i + 1, :] = flat

    x_send.wait_send()
    h_send.wait_send()
    forward.wait_send()
    wait_for(so, g_sem.at[0, 0])
    wait_for(si, g_sem.at[1, 0])
    wait_for(misc_land.at[pl.ds(0, n // 2 - 1)], misc_sem.at[0])
    wait_for(land.at[:, pl.ds(0, n // 2 - 1)], land_sem.at[0])
    wait_for(last_land.at[:, pl.ds(0, n - 1)], last_sem.at[0])
    wait_for(f_land.at[pl.ds(0, n - 1)], f_sem.at[1])
    sums = f_land[0]
    for d in range(1, n):
        sums = sums + f_land[d]
    for i in range(kinds + 1):
        size = float(rows_of[i] * cols_of[i])
        clip = jnp.maximum(1.0, jnp.sqrt(at_lane(sums, i) / size) / rms)
        move = step * jnp.maximum(EPS_TWO, jnp.sqrt(at_lane(sums, kinds + 1 + i) / size))
        coef[i:i + 1, :] = jnp.broadcast_to(move / clip, (1, LANES))
    wait_for(f_land.at[pl.ds(0, n - 1)], f_sem.at[0])


def scalars_kernel(first, *refs):
    lane = lax.broadcasted_iota(jnp.int32, (8, LANES), 1)
    row = jnp.zeros((8, LANES), F32)
    for i, ref in enumerate(refs[:-1]):
        row = jnp.where(lane == first + i, ref[...], row)
    refs[-1][...] = row


def apply_kernel(gi, go, wi, wo, ri, ci, ro, co, coef, ai, ao, colf, wi_out, ri_out, ci_out, wo_out, ro_out, co_out, wi_new, wo_new, sems):
    kinds, m_in, cols_in = wi.shape
    per_in, per_out = gi.shape[0] // kinds, go.shape[0]
    lanes = STRIPE // LANES
    copies = []

    def send(src, dst):
        copies.append(pltpu.make_async_copy(src, dst, sems.at[len(copies)]))
        copies[-1].start()

    def blocks(factor, g, p, c, old, new, out, first):
        for r in range(lanes):
            cols = pl.ds(first + r * LANES, LANES)
            new[:, cols] = old[:, cols] - (factor * colf[c, lanes * p + r]) * g[:, r * LANES:(r + 1) * LANES]
        part = pl.ds(first, STRIPE)
        send(new.at[:, part], out.at[:, part])

    for c in range(2):
        factor = ao[...] * coef[kinds:kinds + 1, :]
        for s in range(per_out):
            blocks(factor, go.at[s, c], s, c, wo, wo_new, wo_out, c * (wo.shape[1] // 2) + s * STRIPE)
    send(ri, ri_out)
    send(ci, ci_out)
    send(ro, ro_out)
    send(co, co_out)
    for k in range(kinds):
        factor = ai[k] * coef[k:k + 1, :]
        for c in range(2):
            for s in range(per_in):
                t = k * per_in + s
                blocks(factor, gi.at[t, c], per_out + t, c, wi.at[k], wi_new.at[k], wi_out.at[k], c * (cols_in // 2) + s * STRIPE)
    for copy in copies:
        copy.wait()


def solution(mesh):
    n = mesh.shape['tp']

    def local_step(x_norm, hid_act, dy_in, dy_out, w_in, w_out, row_in, col_in, row_out, col_out, beta_two, rel_step, clip_rms, clip_norm):
        kinds, m_in, cols_in = w_in.shape
        m_out, cols_out = w_out.shape
        tokens = x_norm.shape[0]
        inside = pl.BlockSpec(memory_space=pltpu.VMEM)
        scalars = lax.cond(
            lax.axis_index('tp') == 0,
            lambda *values: pl.pallas_call(
                lambda *refs: scalars_kernel(kinds + 1, *refs), out_shape=jax.ShapeDtypeStruct((8, LANES), F32),
                in_specs=[inside] * 4, out_specs=inside, name='scalars')(*[v.reshape(1, 1) for v in values]),
            lambda *values: jnp.zeros((8, LANES), F32),
            beta_two, clip_norm, rel_step, clip_rms)
        n_in, n_out = kinds * cols_in // (2 * STRIPE), cols_out // (2 * STRIPE)
        stripes = n_in + n_out
        early = stripes - LAST
        slots = 10
        ins = [x_norm.T, hid_act.T, dy_in, dy_out, w_in, w_out, row_in, col_in, row_out.reshape(1, -1), col_out.reshape(-1, LANES)]
        ins.append(scalars)
        outs = [(n_in, 2, m_in, STRIPE), (n_out, 2, m_out, STRIPE), w_in.shape, w_out.shape, row_in.shape, col_in.shape,
                (1, m_out), (cols_out // LANES, LANES), (8, LANES), (kinds, m_in, LANES), (m_out, LANES), (2, stripes * STRIPE // LANES, 1, LANES)]
        vmem = [((2 * m_in, tokens), jnp.bfloat16), ((2 * m_out, tokens), jnp.bfloat16), ((slots, tokens, STRIPE), jnp.bfloat16),
                ((n_in, m_in, STRIPE), F32), ((n_out, m_out, STRIPE), F32), ((1 + 2 * stripes, 2, LANES), F32),
                ((early, n // 2, 2, 2, LANES), F32), ((n // 2, 2, LANES), F32), ((LAST, n, 2, 2, LANES), F32), ((2, 1 + 2 * stripes, 2, LANES), F32),
                ((1, LANES), F32), ((n, 1, LANES), F32),
                (row_in.shape, F32), (col_in.shape, F32), ((1, m_out), F32), ((cols_out // LANES, LANES), F32)]
        vmem.append(((8, LANES), F32))
        sems = [(slots,), (2,), (2,), (5,), (2, 2), (2, 2), (2,), (2,), (2,), (2,), (2,)]
        anywhere = pl.BlockSpec(memory_space=pl.ANY)
        mid = pl.pallas_call(
            lambda *refs: grads_kernel(n, *refs),
            out_shape=[pltpu.VMEM(s, F32) for s in outs],
            in_specs=[anywhere] * len(ins),
            out_specs=[inside] * len(outs),
            scratch_shapes=[pltpu.VMEM(*v) for v in vmem] + [pltpu.SemaphoreType.DMA(s) for s in sems],
            compiler_params=pltpu.CompilerParams(collective_id=0, has_side_effects=True, vmem_limit_bytes=56 * 2**20),
            name='grads',
        )(*ins)
        finals = [w_in.shape, row_in.shape, col_in.shape, w_out.shape, (1, m_out), (cols_out // LANES, LANES)]
        new = pl.pallas_call(
            apply_kernel,
            out_shape=[jax.ShapeDtypeStruct(s, F32) for s in finals],
            in_specs=[inside] * len(mid),
            out_specs=[anywhere] * len(finals),
            scratch_shapes=[pltpu.VMEM(w_in.shape, F32), pltpu.VMEM(w_out.shape, F32), pltpu.SemaphoreType.DMA((2 * stripes + 4,))],
            compiler_params=pltpu.CompilerParams(vmem_limit_bytes=8 * 2**20),
            name='apply',
        )(*mid)
        return (new[0], new[1], new[2], new[3], new[4].reshape(m_out), new[5].reshape(cols_out))

    in_specs = (P(None, 'tp'), P(None, 'tp'), P(), P(), P(None, 'tp', None), P('tp', None),
                P(None, 'tp'), P(), P('tp'), P(), P(), P(), P(), P())
    out_specs = (P(None, 'tp', None), P(None, 'tp'), P(), P('tp', None), P('tp'), P())
    return jax.shard_map(local_step, mesh=mesh, in_specs=in_specs, out_specs=out_specs, check_vma=False)
```

time: 39.6 us -> 33.7 us (0.85)
  Pallas kernels: 36.2 us -> 32.9 us
  between operations: 3.23 us -> 0.65 us
    pallas_call x1, Pallas kernels: 33.8 us -> 27.9 us  [local_step(): pl.pallas_call(lambda *refs: grads_kernel(n, *refs), out_shape=[pltpu.VME...]
    pallas_call x0 -> x1, Pallas kernels: none -> 2.66 us  [local_step(): pl.pallas_call(lambda *refs: scalars_kernel(kinds + 1, *refs), out_shape=...]
where the time goes in v3:
time: 33.7 us; the launch traced here: 33.5 us
  Pallas kernels  32.9 us (98%)
  between operations  0.65 us (2%)
    pallas_call x1, Pallas kernels, local_step(): pl.pallas_call(lambda *refs: grads_kernel(n, *refs), out_shape=[pltpu.VME...  27.9 us
    pallas_call x1, Pallas kernels, local_step(): pl.pallas_call(lambda *refs: scalars_kernel(kinds + 1, *refs), out_shape=...  2.66 us
    pallas_call x1, Pallas kernels, local_step(): pl.pallas_call(apply_kernel, out_shape=[jax.ShapeDtypeStruct(s, F32) for...  2.25 us

profile of v3, /device:TPU:0, one launch (start us, length us, event | category | flops | bytes accessed | tf_op | source)
XLA Modules:
  0.0 33.5 jit_solution(12672206513631809119)
XLA Ops:
  0.6 2.7 %conditional.1 = (f32[8,128]{1,0:T(8,128)S(1)}) conditional(s32[]{:T(128)} %convert_element_type.3, () %tuple.14, (f32[]{:T(128)}, f32[]{:T(128)}, f32[]{:T(128)}, f32[]{:T(128)}) %tuple.15), branch_computations={%region_0.0_spmd, %region_1.0_spmd} | conditional | bytes 4108 | solution.py:369
  0.7 2.7 %scalars.1 = f32[8,128]{1,0:T(8,128)S(1)} custom-call(f32[1,1]{1,0:T(1,128)} %bitcast.refs_0_, f32[1,1]{1,0:T(1,128)} %bitcast.1.refs_1_, f32[1,1]{1,0:T(1,128)} %bitcast.2.refs_2_, f32[1,1]{1,0:T(1,128)} %bitcast.3.refs_3_), custom_call_target="tpu_custom_call" | custom-call | tf_op jit(solution)/shard_map/cond/branch_1_fun/scalars/pallas_call | solution.py:371
  3.3 27.9 %grads.1 = (f32[10,2,64,512]{3,2,1,0:T(8,128)S(1)}, f32[2,2,160,512]{3,2,1,0:T(8,128)S(1)}, f32[2,64,5120]{2,1,0:T(8,128)S(1)}, f32[160,2048]{1,0:T(8,128)S(1)},...) custom-call(bf16[64,4096]{1,0:T(8,128)(2,1)} %bitcast.11, ...), custom_call_target="tpu_custom_call" | custom-call | tf_op jit(solution)/shard_map/grads/pallas_call | solution.py:392
  31.3 2.3 %apply.1 = (f32[2,64,5120]{2,1,0:T(8,128)}, f32[2,64]{1,0:T(2,128)}, f32[2,5120]{1,0:T(2,128)}, f32[160,2048]{1,0:T(8,128)}, f32[1,160]{1,0:T(1,128)}, /*index=5*/f32[16,128]{1,0:T(8,128)}) custom-call(f32[10,2,64,512]{3,2,1,0:T(8,128)S(1)} %get-tuple-element.39.gi, f32[2,2,160,512]{3,2,1,0:T(8,128)S(1)} %get-tuple-element.40.go, ...), custom_call_target="tpu_custom_call" | custom-call | tf_op jit(solution)/shard_map/apply/pallas_call | solution.py:402

commit v4 on v3

--- a/solution.py
+++ b/solution.py
@@ -10,7 +10,6 @@
 LANES = 128
 STRIPE = 512
 HALF = STRIPE // 2
-LAST = 2
 F32 = jnp.float32
 MESH = pl.DeviceIdType.MESH
 
@@ -18,32 +17,37 @@
 def grads_kernel(n, x_hbm, h_hbm, dyi_hbm, dyo_hbm, wi_hbm, wo_hbm, ri_hbm, ci_hbm, ro_hbm, co_hbm,
                  scal_hbm,
                  gi, go, wi, wo, ri_new, ci_new, ro_new, co_new, coef, ai, ao, colf,
-                 xs, hs, dy, si, so, csend, land, misc_land, last_land, csum,
+                 xs, hs, dy, si, so, csend, land, mid_land, misc_land, last_land, csum, ri_sq, ro_sq, ri_got, ro_got, split,
                  fsend, f_land, ri, ci, ro, co, scal,
-                 dy_sem, x_sem, w_sem, small_sem, xs_sem, g_sem, land_sem, misc_sem, last_sem, fwd_sem, f_sem):
+                 dy_sem, x_sem, w_sem, small_sem, xs_sem, g_sem, land_sem, mid_sem, misc_sem, last_sem, fwd_sem, row_sem, f_sem):
     me = lax.axis_index('tp')
     core = lax.rem(me, 2)
     chip = me // 2
     x, y, z = lax.rem(chip, 2), lax.rem(chip // 2, 2), chip // 4
     partner = me + 1 - 2 * core
-    peers = {0: [], 1: []}
-    for dz in (2, 1, 3, 0):
-        for dy_ in (1, 0):
-            for dx in (1, 0):
-                for dc in (0, 1):
-                    if dz or dy_ or dx or dc:
-                        peers[dc].append(((lax.rem(z + dz, n // 8) * 2 + lax.rem(y + dy_, 2)) * 2 + lax.rem(x + dx, 2)) * 2
-                                         + lax.rem(core + dc, 2))
-    same = peers[0]
-    everyone = [p for pair in zip(peers[0] + [None], peers[1]) for p in pair if p is not None]
+    high = z // 2
+    planes = [3 * (1 - high), 2 - high, z + 1 - 2 * lax.rem(z, 2), z]
+    same, everyone = [], []
+    for plane in planes:
+        for far_y in (1, 0):
+            for far_x in (1, 0):
+                for other in (0, 1):
+                    if plane is z and not (far_y or far_x or other):
+                        continue
+                    place = (plane * 2 + lax.rem(y + far_y, 2)) * 2 + lax.rem(x + far_x, 2)
+                    everyone.append(2 * place + lax.rem(core + other, 2))
+                    if not other:
+                        same.append(everyone[-1])
     kinds, m_in, cols_in = wi.shape
     m_out, cols_out = wo.shape
     half_in, half_out = cols_in // 2, cols_out // 2
     per_in, per_out = half_in // STRIPE, half_out // STRIPE
     n_in = kinds * per_in
     stripes = n_in + per_out
-    slots = dy.shape[0]
-    early = land.shape[0]
+    slots, tokens = dy.shape[0:2]
+    early = 2 * land.shape[0]
+    single = mid_land.shape[0]
+    shared = early + single
 
     def remote(src, dst, sems, peer):
         return pltpu.make_async_remote_copy(src_ref=src, dst_ref=dst, send_sem=sems.at[0], recv_sem=sems.at[1],
@@ -64,6 +68,13 @@
         slot = lax.rem(t + per_out, slots)
         cols = pl.ds(pl.multiple_of(core * half_in + lax.rem(t, per_in) * STRIPE, LANES), STRIPE)
         return pltpu.make_async_copy(dyi_hbm.at[t // per_in, :, cols], dy.at[slot], dy_sem.at[slot])
+
+    def last_copy(part):
+        t = n_in - 1
+        slot = (t + per_out) % slots
+        some = pl.ds(part * (tokens // 2), tokens // 2)
+        cols = pl.ds(pl.multiple_of(core * half_in + t % per_in * STRIPE, LANES), STRIPE)
+        return pltpu.make_async_copy(dyi_hbm.at[t // per_in, some, cols], dy.at[slot, some, :], dy_sem.at[slot + part * slots])
 
     barrier = pltpu.get_barrier_semaphore()
     x_copy = pltpu.make_async_copy(x_hbm, xs.at[pl.ds(0, m_in)], x_sem.at[0])
@@ -86,30 +97,37 @@
             where = (1 + 2 * p + h, pl.ds(r, 1), slice(None))
             csend[where] = csend[where] + part if add else part
 
-    def share(p):
-        mine = csend.at[pl.ds(1 + 2 * p, 2)]
-        to_all(mine, land.at[p, chip], land_sem, same)
-        land[p, chip] = mine[...]
-
+    def share(pair):
+        mine = csend.at[pl.ds(1 + 4 * pair, 4)]
+        to_all(mine, land.at[pair, chip], land_sem, same)
+        land[pair, chip] = mine[...]
+
+    def add_rows(ref, where, sq):
+        ref[where] = ref[where] + (sq[:, 0:LANES] + sq[:, LANES:HALF])
+
+    ri_sq[...] = jnp.zeros_like(ri_sq)
+    ro_sq[...] = jnp.zeros_like(ro_sq)
     x_copy.wait()
     h_copy.wait()
     in_copy(0).start()
     in_copy(1).start()
+    in_copy(2).start()
     pl.semaphore_wait(barrier, n - 1)
     h_send = remote(hs.at[pl.ds(0, m_out)], hs.at[pl.ds(m_out, m_out)], xs_sem.at[1], partner)
     x_send = remote(xs.at[pl.ds(0, m_in)], xs.at[pl.ds(m_in, m_in)], xs_sem.at[0], partner)
+    x_send.start()
     h_send.start()
-    x_send.start()
 
     for s in range(per_out):
         out_copy(s).wait()
-        in_copy(s + 2).start()
+        in_copy(s + 3).start()
         for h in range(2):
             cols = pl.ds(h * HALF, HALF)
             own = jnp.dot(hs[0:m_out, :], dy[s, :, cols], preferred_element_type=F32)
             go[s, core, :, cols] = own
-            put_cols(s, h, jnp.sum(own * own, axis=0, keepdims=True), False)
-    in_copy(4).start()
+            own = own * own
+            put_cols(s, h, jnp.sum(own, axis=0, keepdims=True), False)
+            add_rows(ro_sq, (pl.ds(0, m_out), slice(None)), own)
     for copy in small:
         copy.wait()
     lane = lax.broadcasted_iota(jnp.int32, (1, LANES), 1)
@@ -125,83 +143,128 @@
                             + [jnp.sum(ro[...], axis=1, keepdims=True)]) + scal[0:1, :]
     to_all(csend.at[0], misc_land.at[chip], misc_sem, same)
     misc_land[chip] = csend[0]
-    h_send.wait_recv()
+    x_send.wait_recv()
     in_copy(5).start()
     ahead = 6
-    for s in range(per_out):
+
+    def partner_rows():
+        h_send.wait_recv()
+        for s in range(per_out):
+            for h in range(2):
+                cols = pl.ds(h * HALF, HALF)
+                other = jnp.dot(hs[m_out:2 * m_out, :], dy[s, :, cols], preferred_element_type=F32)
+                so[s, :, cols] = other
+                other = other * other
+                put_cols(s, h, jnp.sum(other, axis=0, keepdims=True), True)
+                add_rows(ro_sq, (pl.ds(m_out, m_out), slice(None)), other)
+        remote(so, go.at[:, core], g_sem.at[0], partner).start()
+        remote(ro_sq.at[pl.ds(m_out, m_out)], ro_got, row_sem.at[0], partner).start()
+        share(0)
+
+    def product(t):
+        p = t + per_out
         for h in range(2):
             cols = pl.ds(h * HALF, HALF)
-            other = jnp.dot(hs[m_out:2 * m_out, :], dy[s, :, cols], preferred_element_type=F32)
-            so[s, :, cols] = other
-            put_cols(s, h, jnp.sum(other * other, axis=0, keepdims=True), True)
-        remote(so.at[s], go.at[s, core], g_sem.at[0], partner).start()
-        share(s)
-    x_send.wait_recv()
-
-    def in_step(t, carry):
+            both = jnp.dot(xs[...], dy[lax.rem(p, slots), :, cols], preferred_element_type=F32)
+            gi[t, core, :, cols] = both[0:m_in]
+            si[t, :, cols] = both[m_in:2 * m_in]
+            both = both * both
+            put_cols(p, h, jnp.sum(both, axis=0, keepdims=True), False)
+            add_rows(ri_sq, t // per_in, both)
+
+    def give(t, size):
+        remote(si.at[pl.ds(t, size)], gi.at[pl.ds(t, size), core], g_sem.at[1], partner).start()
+
+    def in_step(i, carry):
+        @pl.when(i == 1)
+        def _():
+            partner_rows()
+
+        for t in (2 * i, 2 * i + 1):
+            in_copy(t).wait()
+
+            @pl.when(t + ahead < n_in - 1)
+            def _():
+                in_copy(t + ahead).start()
+
+            @pl.when(t + ahead == n_in - 1)
+            def _():
+                for h in range(2):
+                    last_copy(h).start()
+
+        for t in (2 * i, 2 * i + 1):
+            product(t)
+        share(i + 1)
+        give(2 * i, 2)
+        return carry
+
+    lax.fori_loop(0, early // 2 - 1, in_step, 0)
+    def single_step(t, carry):
         in_copy(t).wait()
-
-        @pl.when(t + ahead < n_in)
-        def _():
-            in_copy(t + ahead).start()
-
+        product(t)
         p = t + per_out
-        slot = lax.rem(p, slots)
+        mine = csend.at[pl.ds(1 + 2 * p, 2)]
+        to_all(mine, mid_land.at[p - early, chip], mid_sem, same)
+        mid_land[p - early, chip] = mine[...]
+        give(t, 1)
+        return carry
+
+    lax.fori_loop(early - per_out, n_in - 1, single_step, 0)
+    t = n_in - 1
+    last_copy(0).wait()
+    for part in range(2):
+        some = pl.ds(part * (tokens // 2), tokens // 2)
+        if part:
+            last_copy(1).wait()
+            wi_copy = pltpu.make_async_copy(wi_hbm, wi, w_sem.at[0])
+            wo_copy = pltpu.make_async_copy(wo_hbm, wo, w_sem.at[1])
+            wi_copy.start()
+            wo_copy.start()
         for h in range(2):
             cols = pl.ds(h * HALF, HALF)
-            both = jnp.dot(xs[...], dy[slot, :, cols], preferred_element_type=F32)
+            both = jnp.dot(xs[:, some], dy[(t + per_out) % slots, some, cols], preferred_element_type=F32)
+            if not part:
+                split[h] = both
+                continue
+            both = split[h] + both
             gi[t, core, :, cols] = both[0:m_in]
             si[t, :, cols] = both[m_in:2 * m_in]
-            put_cols(p, h, jnp.sum(both * both, axis=0, keepdims=True), False)
-
-        @pl.when(p < early)
-        def _():
-            share(p)
-
-        @pl.when(p >= early)
-        def _():
-            mine = csend.at[pl.ds(1 + 2 * p, 2)]
-            to_all(mine, last_land.at[p - early, me], last_sem, everyone)
-            last_land[p - early, me] = mine[...]
-
-        remote(si.at[t], gi.at[t, core], g_sem.at[1], partner).start()
-        return carry
-
-    lax.fori_loop(0, n_in, in_step, 0)
-    wi_copy = pltpu.make_async_copy(wi_hbm, wi, w_sem.at[0])
-    wo_copy = pltpu.make_async_copy(wo_hbm, wo, w_sem.at[1])
-    wi_copy.start()
-    wo_copy.start()
-
-    wait_for(so, g_sem.at[0, 1])
-    wait_for(si, g_sem.at[1, 1])
-
-    def row_sq(ref, blocks):
-        rows = ref.shape[2]
-
-        def add(t, total):
-            for c in range(2):
-                for r in range(STRIPE // LANES):
-                    g = ref[t, c, :, r * LANES:(r + 1) * LANES]
-                    total = total + g * g
-            return total
-
-        return jnp.sum(lax.fori_loop(blocks[0], blocks[1], add, jnp.zeros((rows, LANES), F32)), axis=1, keepdims=True)
-
-    row_sums = [row_sq(gi, (k * per_in, (k + 1) * per_in)) for k in range(kinds)] + [row_sq(go, (0, per_out))]
-
+            both = both * both
+            put_cols(t + per_out, h, jnp.sum(both, axis=0, keepdims=True), False)
+            add_rows(ri_sq, t // per_in, both)
+    mine = csend.at[pl.ds(1 + 2 * shared, 2)]
+    to_all(mine, last_land.at[me], last_sem, everyone)
+    last_land[me] = mine[...]
+    remote(ri_sq.at[:, pl.ds(m_in, m_in)], ri_got, row_sem.at[1], partner).start()
+    give(n_in - 1, 1)
     wait_for(misc_land.at[pl.ds(0, n // 2 - 1)], misc_sem.at[1])
     wait_for(land.at[:, pl.ds(0, n // 2 - 1)], land_sem.at[1])
     csum[core, 0] = jnp.sum(misc_land[...], axis=0)
-    for p in range(early):
-        csum[core, pl.ds(1 + 2 * p, 2)] = jnp.sum(land[p], axis=0)
-    done = csum.at[core, pl.ds(0, 1 + 2 * early)]
+    for pair in range(early // 2):
+        csum[core, pl.ds(1 + 4 * pair, 4)] = jnp.sum(land[pair], axis=0)
+    wait_for(mid_land.at[:, pl.ds(0, n // 2 - 1)], mid_sem.at[1])
+    for i in range(single):
+        csum[core, pl.ds(1 + 2 * (early + i), 2)] = jnp.sum(mid_land[i], axis=0)
+    done = csum.at[core, pl.ds(0, 1 + 2 * shared)]
     forward = remote(done, done, fwd_sem, partner)
     forward.start()
+    wait_for(ro_got, row_sem.at[0, 1])
+    wait_for(ri_got, row_sem.at[1, 1])
+    row_sums = [jnp.sum(ri_sq[k, 0:m_in] + ri_got[k], axis=1, keepdims=True) for k in range(kinds)]
+    row_sums.append(jnp.sum(ro_sq[0:m_out] + ro_got[...], axis=1, keepdims=True))
+    def square_sum(ref, cols):
+        rows = ref.shape[0]
+        total = [jnp.zeros((8, LANES), F32) for _ in range(4)]
+        for r in range(cols // LANES):
+            for b in range(rows // 8):
+                w = ref[8 * b:8 * (b + 1), r * LANES:(r + 1) * LANES]
+                total[b % 4] = total[b % 4] + w * w
+        total = (total[0] + total[1]) + (total[2] + total[3])
+        return jnp.sum(jnp.sum(total, axis=0, keepdims=True), axis=1, keepdims=True)
+
     wi_copy.wait()
     wo_copy.wait()
-    w_sums = [jnp.sum(jnp.sum(wi[k] * wi[k], axis=0, keepdims=True), axis=1, keepdims=True) for k in range(kinds)]
-    w_sums.append(jnp.sum(jnp.sum(wo[...] * wo[...], axis=0, keepdims=True), axis=1, keepdims=True))
+    w_sums = [square_sum(wi.at[k], cols_in) for k in range(kinds)] + [square_sum(wo, cols_out)]
     forward.wait_recv()
     first = [1 + 2 * (per_out + k * per_in) for k in range(kinds)] + [1]
     count = [2 * per_in] * kinds + [2 * per_out]
@@ -221,16 +284,15 @@
         old = ro[...] if i == kinds else ri[i:i + 1, :]
         olds.append(keep * jnp.sum(jnp.where(eyes[i], old, 0.0), axis=1, keepdims=True))
         levels.append(keep * (at_lane(misc, i) / rows_of[i]))
-        known = min(first[i] + count[i], 1 + 2 * early)
+        known = min(first[i] + count[i], 1 + 2 * shared)
         grand.append(jnp.sum(csum[:, first[i]:known], axis=(0, 1)))
-    wait_for(last_land.at[:, pl.ds(0, n - 1)], last_sem.at[1])
-    for stripe in range(stripes - early):
-        for c in range(2):
-            total = last_land[stripe, c]
-            for q in range(1, n // 2):
-                total = total + last_land[stripe, 2 * q + c]
-            csum[c, pl.ds(1 + 2 * (early + stripe), 2)] = total
-            grand[kinds - 1] = grand[kinds - 1] + jnp.sum(total, axis=0)
+    wait_for(last_land.at[pl.ds(0, n - 1)], last_sem.at[1])
+    for c in range(2):
+        total = last_land[c]
+        for q in range(1, n // 2):
+            total = total + last_land[2 * q + c]
+        csum[c, pl.ds(1 + 2 * shared, 2)] = total
+        grand[kinds - 1] = grand[kinds - 1] + jnp.sum(total, axis=0)
     grand = [jnp.sum(jnp.sum(g, axis=0, keepdims=True), axis=1, keepdims=True) for g in grand]
     norm_sq = grand[0]
     for g in grand[1:]:
@@ -264,6 +326,8 @@
                 store[spot] = new
                 colf[c, STRIPE // LANES * p + r] = lax.rsqrt(new)
 
+    wait_for(so, g_sem.at[0, 1])
+    wait_for(si, g_sem.at[1, 1])
     def update_sq(ref, factor, p0, blocks):
         rows = ref.shape[2]
 
@@ -279,7 +343,7 @@
                     total = total + fold * (col * col)
             return total
 
-        total = lax.fori_loop(blocks[0], blocks[1], add, jnp.zeros((8, LANES), F32))
+        total = lax.fori_loop(blocks[0], blocks[1], add, jnp.zeros((8, LANES), F32), unroll=True)
         return jnp.sum(jnp.sum(total, axis=0, keepdims=True), axis=1, keepdims=True)
 
     u_sums = [update_sq(gi, ai[k], per_out, (k * per_in, (k + 1) * per_in)) for k in range(kinds)]
@@ -302,7 +366,10 @@
     wait_for(si, g_sem.at[1, 0])
     wait_for(misc_land.at[pl.ds(0, n // 2 - 1)], misc_sem.at[0])
     wait_for(land.at[:, pl.ds(0, n // 2 - 1)], land_sem.at[0])
-    wait_for(last_land.at[:, pl.ds(0, n - 1)], last_sem.at[0])
+    wait_for(mid_land.at[:, pl.ds(0, n // 2 - 1)], mid_sem.at[0])
+    wait_for(ro_got, row_sem.at[0, 0])
+    wait_for(ri_got, row_sem.at[1, 0])
+    wait_for(last_land.at[pl.ds(0, n - 1)], last_sem.at[0])
     wait_for(f_land.at[pl.ds(0, n - 1)], f_sem.at[1])
     sums = f_land[0]
     for d in range(1, n):
@@ -315,12 +382,9 @@
     wait_for(f_land.at[pl.ds(0, n - 1)], f_sem.at[0])
 
 
-def scalars_kernel(first, *refs):
+def scalar_kernel(place, one, two, row):
     lane = lax.broadcasted_iota(jnp.int32, (8, LANES), 1)
-    row = jnp.zeros((8, LANES), F32)
-    for i, ref in enumerate(refs[:-1]):
-        row = jnp.where(lane == first + i, ref[...], row)
-    refs[-1][...] = row
+    row[...] = jnp.where(lane == place, one[...], jnp.where(lane == place + 1, two[...], 0.0))
 
 
 def apply_kernel(gi, go, wi, wo, ri, ci, ro, co, coef, ai, ao, colf, wi_out, ri_out, ci_out, wo_out, ro_out, co_out, wi_new, wo_new, sems):
@@ -366,16 +430,17 @@
         m_out, cols_out = w_out.shape
         tokens = x_norm.shape[0]
         inside = pl.BlockSpec(memory_space=pltpu.VMEM)
-        scalars = lax.cond(
-            lax.axis_index('tp') == 0,
-            lambda *values: pl.pallas_call(
-                lambda *refs: scalars_kernel(kinds + 1, *refs), out_shape=jax.ShapeDtypeStruct((8, LANES), F32),
-                in_specs=[inside] * 4, out_specs=inside, name='scalars')(*[v.reshape(1, 1) for v in values]),
-            lambda *values: jnp.zeros((8, LANES), F32),
+        scalars = lax.switch(
+            jnp.minimum(lax.axis_index('tp'), 2),
+            [lambda *values, i=i: pl.pallas_call(
+                lambda *refs: scalar_kernel(kinds + 1 + 2 * i, *refs), out_shape=jax.ShapeDtypeStruct((8, LANES), F32),
+                in_specs=[inside] * 2, out_specs=inside, name='scalar')(*[v.reshape(1, 1) for v in values[2 * i:2 * i + 2]]) for i in range(2)]
+            + [lambda *values: jnp.zeros((8, LANES), F32)],
             beta_two, clip_norm, rel_step, clip_rms)
         n_in, n_out = kinds * cols_in // (2 * STRIPE), cols_out // (2 * STRIPE)
         stripes = n_in + n_out
-        early = stripes - LAST
+        single = 3
+        early = stripes - single - 1
         slots = 10
         ins = [x_norm.T, hid_act.T, dy_in, dy_out, w_in, w_out, row_in, col_in, row_out.reshape(1, -1), col_out.reshape(-1, LANES)]
         ins.append(scalars)
@@ -383,11 +448,12 @@
                 (1, m_out), (cols_out // LANES, LANES), (8, LANES), (kinds, m_in, LANES), (m_out, LANES), (2, stripes * STRIPE // LANES, 1, LANES)]
         vmem = [((2 * m_in, tokens), jnp.bfloat16), ((2 * m_out, tokens), jnp.bfloat16), ((slots, tokens, STRIPE), jnp.bfloat16),
                 ((n_in, m_in, STRIPE), F32), ((n_out, m_out, STRIPE), F32), ((1 + 2 * stripes, 2, LANES), F32),
-                ((early, n // 2, 2, 2, LANES), F32), ((n // 2, 2, LANES), F32), ((LAST, n, 2, 2, LANES), F32), ((2, 1 + 2 * stripes, 2, LANES), F32),
+                ((early // 2, n // 2, 4, 2, LANES), F32), ((single, n // 2, 2, 2, LANES), F32), ((n // 2, 2, LANES), F32), ((n, 2, 2, LANES), F32), ((2, 1 + 2 * stripes, 2, LANES), F32),
+                ((kinds, 2 * m_in, LANES), F32), ((2 * m_out, LANES), F32), ((kinds, m_in, LANES), F32), ((m_out, LANES), F32), ((2, 2 * m_in, HALF), F32),
                 ((1, LANES), F32), ((n, 1, LANES), F32),
                 (row_in.shape, F32), (col_in.shape, F32), ((1, m_out), F32), ((cols_out // LANES, LANES), F32)]
         vmem.append(((8, LANES), F32))
-        sems = [(slots,), (2,), (2,), (5,), (2, 2), (2, 2), (2,), (2,), (2,), (2,), (2,)]
+        sems = [(2 * slots,), (2,), (2,), (5,), (2, 2), (2, 2), (2,), (2,), (2,), (2,), (2,), (2, 2), (2,)]
         anywhere = pl.BlockSpec(memory_space=pl.ANY)
         mid = pl.pallas_call(
             lambda *refs: grads_kernel(n, *refs),

time: 33.7 us -> 32.8 us (0.973)
  Pallas kernels: 32.9 us -> 32 us
    pallas_call x1, Pallas kernels: 2.66 us -> 1.37 us  [local_step(): pl.pallas_call(lambda *refs: scalar_kernel(kinds + 1 + 2 * i, *refs), out...]
    pallas_call x1, Pallas kernels: 27.9 us -> 28.4 us  [local_step(): pl.pallas_call(lambda *refs: grads_kernel(n, *refs), out_shape=[pltpu.VME...]
where the time goes in v4:
time: 32.8 us; the launch traced here: 32.6 us
  Pallas kernels  32 us (98%)
  between operations  0.65 us (2%)
    pallas_call x1, Pallas kernels, local_step(): pl.pallas_call(lambda *refs: grads_kernel(n, *refs), out_shape=[pltpu.VME...  28.4 us
    pallas_call x1, Pallas kernels, local_step(): pl.pallas_call(apply_kernel, out_shape=[jax.ShapeDtypeStruct(s, F32) for...  2.25 us
    pallas_call x1, Pallas kernels, local_step(): pl.pallas_call(lambda *refs: scalar_kernel(kinds + 1 + 2 * i, *refs), out...  1.37 us

profile of v4, /device:TPU:0, one launch (start us, length us, event | category | flops | bytes accessed | tf_op | source)
XLA Modules:
  0.0 32.6 jit_solution(4764386611895821031)
XLA Ops:
  0.6 1.4 %conditional.1 = (f32[8,128]{1,0:T(8,128)S(1)}) conditional(s32[]{:T(128)} %clamp.3, (f32[]{:T(128)}, f32[]{:T(128)}) %tuple.17, (f32[]{:T(128)}, f32[]{:T(128)}) %tuple.18, () %tuple.19), branch_computations={%region_0.0_spmd, %region_1.0_spmd, %region_2.0_spmd} | conditional | bytes 4108 | solution.py:433
  0.6 1.4 %scalar.2 = f32[8,128]{1,0:T(8,128)S(1)} custom-call(f32[1,1]{1,0:T(1,128)} %bitcast.refs_0_, f32[1,1]{1,0:T(1,128)} %bitcast.1.refs_1_), custom_call_target="tpu_custom_call" | custom-call | tf_op jit(solution)/shard_map/cond/branch_0_fun/scalar/pallas_call | solution.py:435
  2.0 28.4 %grads.1 = (f32[10,2,64,512]{3,2,1,0:T(8,128)S(1)}, f32[2,2,160,512]{3,2,1,0:T(8,128)S(1)}, f32[2,64,5120]{2,1,0:T(8,128)S(1)}, f32[160,2048]{1,0:T(8,128)S(1)},...) custom-call(bf16[64,4096]{1,0:T(8,128)(2,1)} %bitcast.11, ...), custom_call_target="tpu_custom_call" | custom-call | tf_op jit(solution)/shard_map/grads/pallas_call | solution.py:458
  30.4 2.3 %apply.1 = (f32[2,64,5120]{2,1,0:T(8,128)}, f32[2,64]{1,0:T(2,128)}, f32[2,5120]{1,0:T(2,128)}, f32[160,2048]{1,0:T(8,128)}, f32[1,160]{1,0:T(1,128)}, /*index=5*/f32[16,128]{1,0:T(8,128)}) custom-call(f32[10,2,64,512]{3,2,1,0:T(8,128)S(1)} %get-tuple-element.40.gi, f32[2,2,160,512]{3,2,1,0:T(8,128)S(1)} %get-tuple-element.41.go, ...), custom_call_target="tpu_custom_call" | custom-call | tf_op jit(solution)/shard_map/apply/pallas_call | solution.py:468

commit v5 on v4

--- a/solution.py
+++ b/solution.py
@@ -10,6 +10,8 @@
 LANES = 128
 STRIPE = 512
 HALF = STRIPE // 2
+PARTS = 4
+AHEAD = 6
 F32 = jnp.float32
 MESH = pl.DeviceIdType.MESH
 
@@ -19,7 +21,7 @@
                  gi, go, wi, wo, ri_new, ci_new, ro_new, co_new, coef, ai, ao, colf,
                  xs, hs, dy, si, so, csend, land, mid_land, misc_land, last_land, csum, ri_sq, ro_sq, ri_got, ro_got, split,
                  fsend, f_land, ri, ci, ro, co, scal,
-                 dy_sem, x_sem, w_sem, small_sem, xs_sem, g_sem, land_sem, mid_sem, misc_sem, last_sem, fwd_sem, row_sem, f_sem):
+                 dy_sem, w_sem, xs_sem, g_sem, land_sem, mid_sem, misc_sem, last_sem, fwd_sem, row_sem, f_sem):
     me = lax.axis_index('tp')
     core = lax.rem(me, 2)
     chip = me // 2
@@ -62,23 +64,23 @@
 
     def out_copy(s):
         cols = pl.ds(pl.multiple_of(core * half_out + s * STRIPE, LANES), STRIPE)
-        return pltpu.make_async_copy(dyo_hbm.at[:, cols], dy.at[s], dy_sem.at[s])
+        return pltpu.make_async_copy(dyo_hbm.at[:, cols], dy.at[s], dy_sem.at[s + AHEAD // 2])
 
     def in_copy(t):
         slot = lax.rem(t + per_out, slots)
         cols = pl.ds(pl.multiple_of(core * half_in + lax.rem(t, per_in) * STRIPE, LANES), STRIPE)
-        return pltpu.make_async_copy(dyi_hbm.at[t // per_in, :, cols], dy.at[slot], dy_sem.at[slot])
+        return pltpu.make_async_copy(dyi_hbm.at[t // per_in, :, cols], dy.at[slot], dy_sem.at[lax.rem(t, AHEAD)])
 
     def last_copy(part):
         t = n_in - 1
         slot = (t + per_out) % slots
-        some = pl.ds(part * (tokens // 2), tokens // 2)
+        some = pl.ds(part * (tokens // PARTS), tokens // PARTS)
         cols = pl.ds(pl.multiple_of(core * half_in + t % per_in * STRIPE, LANES), STRIPE)
-        return pltpu.make_async_copy(dyi_hbm.at[t // per_in, some, cols], dy.at[slot, some, :], dy_sem.at[slot + part * slots])
+        return pltpu.make_async_copy(dyi_hbm.at[t // per_in, some, cols], dy.at[slot, some, :], dy_sem.at[(t + part) % AHEAD])
 
     barrier = pltpu.get_barrier_semaphore()
-    x_copy = pltpu.make_async_copy(x_hbm, xs.at[pl.ds(0, m_in)], x_sem.at[0])
-    h_copy = pltpu.make_async_copy(h_hbm, hs.at[pl.ds(0, m_out)], x_sem.at[1])
+    x_copy = pltpu.make_async_copy(x_hbm, xs.at[pl.ds(0, m_in)], w_sem.at[0])
+    h_copy = pltpu.make_async_copy(h_hbm, hs.at[pl.ds(0, m_out)], w_sem.at[1])
     x_copy.start()
     h_copy.start()
     out_copy(0).start()
@@ -86,8 +88,8 @@
         pl.semaphore_signal(barrier, inc=1, device_id=(peer,), device_id_type=MESH)
     for s in range(1, per_out):
         out_copy(s).start()
-    small = [pltpu.make_async_copy(src, dst, small_sem.at[i]) for i, (src, dst) in enumerate(
-        ((ri_hbm, ri), (ci_hbm, ci), (ro_hbm, ro), (co_hbm, co), (scal_hbm, scal)))]
+    small = [pltpu.make_async_copy(src, dst, sem.at[0]) for src, dst, sem in (
+        (ri_hbm, ri, land_sem), (ci_hbm, ci, mid_sem), (ro_hbm, ro, misc_sem), (co_hbm, co, last_sem), (scal_hbm, scal, fwd_sem))]
     for copy in small:
         copy.start()
 
@@ -145,7 +147,6 @@
     misc_land[chip] = csend[0]
     x_send.wait_recv()
     in_copy(5).start()
-    ahead = 6
 
     def partner_rows():
         h_send.wait_recv()
@@ -183,14 +184,14 @@
         for t in (2 * i, 2 * i + 1):
             in_copy(t).wait()
 
-            @pl.when(t + ahead < n_in - 1)
+            @pl.when(t + AHEAD < n_in - 1)
             def _():
-                in_copy(t + ahead).start()
-
-            @pl.when(t + ahead == n_in - 1)
-            def _():
-                for h in range(2):
-                    last_copy(h).start()
+                in_copy(t + AHEAD).start()
+
+            for part in range(PARTS):
+                @pl.when(t + AHEAD == n_in - 1 + part)
+                def _():
+                    last_copy(part).start()
 
         for t in (2 * i, 2 * i + 1):
             product(t)
@@ -201,6 +202,11 @@
     lax.fori_loop(0, early // 2 - 1, in_step, 0)
     def single_step(t, carry):
         in_copy(t).wait()
+        for part in range(PARTS):
+            @pl.when(t + AHEAD == n_in - 1 + part)
+            def _():
+                last_copy(part).start()
+
         product(t)
         p = t + per_out
         mine = csend.at[pl.ds(1 + 2 * p, 2)]
@@ -211,11 +217,10 @@
 
     lax.fori_loop(early - per_out, n_in - 1, single_step, 0)
     t = n_in - 1
-    last_copy(0).wait()
-    for part in range(2):
-        some = pl.ds(part * (tokens // 2), tokens // 2)
-        if part:
-            last_copy(1).wait()
+    for part in range(PARTS):
+        some = pl.ds(part * (tokens // PARTS), tokens // PARTS)
+        last_copy(part).wait()
+        if part == PARTS - 1:
             wi_copy = pltpu.make_async_copy(wi_hbm, wi, w_sem.at[0])
             wo_copy = pltpu.make_async_copy(wo_hbm, wo, w_sem.at[1])
             wi_copy.start()
@@ -223,10 +228,11 @@
         for h in range(2):
             cols = pl.ds(h * HALF, HALF)
             both = jnp.dot(xs[:, some], dy[(t + per_out) % slots, some, cols], preferred_element_type=F32)
-            if not part:
+            if part:
+                both = split[h] + both
+            if part < PARTS - 1:
                 split[h] = both
                 continue
-            both = split[h] + both
             gi[t, core, :, cols] = both[0:m_in]
             si[t, :, cols] = both[m_in:2 * m_in]
             both = both * both
@@ -391,35 +397,34 @@
     kinds, m_in, cols_in = wi.shape
     per_in, per_out = gi.shape[0] // kinds, go.shape[0]
     lanes = STRIPE // LANES
-    copies = []
-
-    def send(src, dst):
-        copies.append(pltpu.make_async_copy(src, dst, sems.at[len(copies)]))
-        copies[-1].start()
-
-    def blocks(factor, g, p, c, old, new, out, first):
+
+    def send(src, dst, sem):
+        copy = pltpu.make_async_copy(src, dst, sems.at[sem])
+        copy.start()
+        return copy
+
+    def blocks(factor, g, p, c, old, new, out, first, sem):
         for r in range(lanes):
             cols = pl.ds(first + r * LANES, LANES)
             new[:, cols] = old[:, cols] - (factor * colf[c, lanes * p + r]) * g[:, r * LANES:(r + 1) * LANES]
         part = pl.ds(first, STRIPE)
-        send(new.at[:, part], out.at[:, part])
+        send(new.at[:, part], out.at[:, part], sem)
 
     for c in range(2):
         factor = ao[...] * coef[kinds:kinds + 1, :]
         for s in range(per_out):
-            blocks(factor, go.at[s, c], s, c, wo, wo_new, wo_out, c * (wo.shape[1] // 2) + s * STRIPE)
-    send(ri, ri_out)
-    send(ci, ci_out)
-    send(ro, ro_out)
-    send(co, co_out)
+            blocks(factor, go.at[s, c], s, c, wo, wo_new, wo_out, c * (wo.shape[1] // 2) + s * STRIPE, 0)
+    small = [send(src, dst, 2 + i) for i, (src, dst) in enumerate(((ri, ri_out), (ci, ci_out), (ro, ro_out), (co, co_out)))]
     for k in range(kinds):
         factor = ai[k] * coef[k:k + 1, :]
         for c in range(2):
             for s in range(per_in):
                 t = k * per_in + s
-                blocks(factor, gi.at[t, c], per_out + t, c, wi.at[k], wi_new.at[k], wi_out.at[k], c * (cols_in // 2) + s * STRIPE)
-    for copy in copies:
+                blocks(factor, gi.at[t, c], per_out + t, c, wi.at[k], wi_new.at[k], wi_out.at[k], c * (cols_in // 2) + s * STRIPE, 1)
+    for copy in small:
         copy.wait()
+    pltpu.make_async_copy(wo_new, wo_out, sems.at[0]).wait()
+    pltpu.make_async_copy(wi_new, wi_out, sems.at[1]).wait()
 
 
 def solution(mesh):
@@ -453,7 +458,7 @@
                 ((1, LANES), F32), ((n, 1, LANES), F32),
                 (row_in.shape, F32), (col_in.shape, F32), ((1, m_out), F32), ((cols_out // LANES, LANES), F32)]
         vmem.append(((8, LANES), F32))
-        sems = [(2 * slots,), (2,), (2,), (5,), (2, 2), (2, 2), (2,), (2,), (2,), (2,), (2,), (2, 2), (2,)]
+        sems = [(AHEAD,), (2,), (2, 2), (2, 2), (2,), (2,), (2,), (2,), (2,), (2, 2), (2,)]
         anywhere = pl.BlockSpec(memory_space=pl.ANY)
         mid = pl.pallas_call(
             lambda *refs: grads_kernel(n, *refs),
@@ -470,7 +475,7 @@
             out_shape=[jax.ShapeDtypeStruct(s, F32) for s in finals],
             in_specs=[inside] * len(mid),
             out_specs=[anywhere] * len(finals),
-            scratch_shapes=[pltpu.VMEM(w_in.shape, F32), pltpu.VMEM(w_out.shape, F32), pltpu.SemaphoreType.DMA((2 * stripes + 4,))],
+            scratch_shapes=[pltpu.VMEM(w_in.shape, F32), pltpu.VMEM(w_out.shape, F32), pltpu.SemaphoreType.DMA((6,))],
             compiler_params=pltpu.CompilerParams(vmem_limit_bytes=8 * 2**20),
             name='apply',
         )(*mid)

time: 32.8 us -> 32.3 us (0.985)
  Pallas kernels: 32 us -> 31.5 us
where the time goes in v5:
time: 32.3 us; the launch traced here: 32.1 us
  Pallas kernels  31.5 us (98%)
  between operations  0.65 us (2%)
    pallas_call x1, Pallas kernels, local_step(): pl.pallas_call(lambda *refs: grads_kernel(n, *refs), out_shape=[pltpu.VME...  28 us
    pallas_call x1, Pallas kernels, local_step(): pl.pallas_call(apply_kernel, out_shape=[jax.ShapeDtypeStruct(s, F32) for...  2.06 us
    pallas_call x1, Pallas kernels, local_step(): pl.pallas_call(lambda *refs: scalar_kernel(kinds + 1 + 2 * i, *refs), out...  1.37 us

profile of v5, /device:TPU:0, one launch (start us, length us, event | category | flops | bytes accessed | tf_op | source)
XLA Modules:
  0.0 32.1 jit_solution(8249585792426384794)
XLA Ops:
  0.6 1.4 %conditional.1 = (f32[8,128]{1,0:T(8,128)S(1)}) conditional(s32[]{:T(128)} %clamp.3, (f32[]{:T(128)}, f32[]{:T(128)}) %tuple.17, (f32[]{:T(128)}, f32[]{:T(128)}) %tuple.18, () %tuple.19), branch_computations={%region_0.0_spmd, %region_1.0_spmd, %region_2.0_spmd} | conditional | bytes 4108 | solution.py:438
  0.6 1.4 %scalar.2 = f32[8,128]{1,0:T(8,128)S(1)} custom-call(f32[1,1]{1,0:T(1,128)} %bitcast.refs_0_, f32[1,1]{1,0:T(1,128)} %bitcast.1.refs_1_), custom_call_target="tpu_custom_call" | custom-call | tf_op jit(solution)/shard_map/cond/branch_0_fun/scalar/pallas_call | solution.py:440
  2.0 28.0 %grads.1 = (f32[10,2,64,512]{3,2,1,0:T(8,128)S(1)}, f32[2,2,160,512]{3,2,1,0:T(8,128)S(1)}, f32[2,64,5120]{2,1,0:T(8,128)S(1)}, f32[160,2048]{1,0:T(8,128)S(1)},...) custom-call(bf16[64,4096]{1,0:T(8,128)(2,1)} %bitcast.11, ...), custom_call_target="tpu_custom_call" | custom-call | tf_op jit(solution)/shard_map/grads/pallas_call | solution.py:463
  30.1 2.1 %apply.1 = (f32[2,64,5120]{2,1,0:T(8,128)}, f32[2,64]{1,0:T(2,128)}, f32[2,5120]{1,0:T(2,128)}, f32[160,2048]{1,0:T(8,128)}, f32[1,160]{1,0:T(1,128)}, /*index=5*/f32[16,128]{1,0:T(8,128)}) custom-call(f32[10,2,64,512]{3,2,1,0:T(8,128)S(1)} %get-tuple-element.40.gi, f32[2,2,160,512]{3,2,1,0:T(8,128)S(1)} %get-tuple-element.41.go, ...), custom_call_target="tpu_custom_call" | custom-call | tf_op jit(solution)/shard_map/apply/pallas_call | solution.py:473

commit v6 on v5

--- a/solution.py
+++ b/solution.py
@@ -336,24 +336,25 @@
     wait_for(si, g_sem.at[1, 1])
     def update_sq(ref, factor, p0, blocks):
         rows = ref.shape[2]
-
-        def add(t, total):
-            for c in range(2):
-                for r in range(STRIPE // LANES):
-                    part = ref[t, c, :, r * LANES:(r + 1) * LANES] * factor
-                    part = part * part
-                    fold = part[0:8]
-                    for b in range(1, rows // 8):
-                        fold = fold + part[8 * b:8 * (b + 1)]
-                    col = colf[c, STRIPE // LANES * (p0 + t) + r]
-                    total = total + fold * (col * col)
-            return total
-
-        total = lax.fori_loop(blocks[0], blocks[1], add, jnp.zeros((8, LANES), F32), unroll=True)
-        return jnp.sum(jnp.sum(total, axis=0, keepdims=True), axis=1, keepdims=True)
-
-    u_sums = [update_sq(gi, ai[k], per_out, (k * per_in, (k + 1) * per_in)) for k in range(kinds)]
-    u_sums.append(update_sq(go, ao[...], 0, (0, per_out)))
+        spots = [(t, c, r) for t in range(*blocks) for c in range(2) for r in range(STRIPE // LANES)]
+        totals = [None] * len(spots)
+        for b in range(rows // 8):
+            some = slice(8 * b, 8 * (b + 1))
+            weight = factor[some, :]
+            for i, (t, c, r) in enumerate(spots):
+                part = ref[t, c, some, r * LANES:(r + 1) * LANES] * weight
+                part = part * part
+                totals[i] = part if totals[i] is None else totals[i] + part
+        parts = []
+        for (t, c, r), total in zip(spots, totals):
+            col = colf[c, STRIPE // LANES * (p0 + t) + r]
+            parts.append(total * (col * col))
+        while len(parts) > 1:
+            parts = [a + b for a, b in zip(parts[::2], parts[1::2])] + parts[len(parts) // 2 * 2:]
+        return jnp.sum(jnp.sum(parts[0], axis=0, keepdims=True), axis=1, keepdims=True)
+
+    u_sums = [update_sq(gi, ai.at[k], per_out, (k * per_in, (k + 1) * per_in)) for k in range(kinds)]
+    u_sums.append(update_sq(go, ao, 0, (0, per_out)))
     fsend[...] = pack(u_sums + w_sums)
     to_all(fsend, f_land.at[me], f_sem, everyone)
     f_land[me] = fsend[...]
@@ -377,9 +378,10 @@
     wait_for(ri_got, row_sem.at[1, 0])
     wait_for(last_land.at[pl.ds(0, n - 1)], last_sem.at[0])
     wait_for(f_land.at[pl.ds(0, n - 1)], f_sem.at[1])
-    sums = f_land[0]
-    for d in range(1, n):
-        sums = sums + f_land[d]
+    parts = [f_land[d] for d in range(n)]
+    while len(parts) > 1:
+        parts = [a + b for a, b in zip(parts[::2], parts[1::2])]
+    sums = parts[0]
     for i in range(kinds + 1):
         size = float(rows_of[i] * cols_of[i])
         clip = jnp.maximum(1.0, jnp.sqrt(at_lane(sums, i) / size) / rms)
@@ -410,11 +412,11 @@
         part = pl.ds(first, STRIPE)
         send(new.at[:, part], out.at[:, part], sem)
 
+    small = [send(src, dst, 2 + i) for i, (src, dst) in enumerate(((ri, ri_out), (ci, ci_out), (ro, ro_out), (co, co_out)))]
     for c in range(2):
         factor = ao[...] * coef[kinds:kinds + 1, :]
         for s in range(per_out):
             blocks(factor, go.at[s, c], s, c, wo, wo_new, wo_out, c * (wo.shape[1] // 2) + s * STRIPE, 0)
-    small = [send(src, dst, 2 + i) for i, (src, dst) in enumerate(((ri, ri_out), (ci, ci_out), (ro, ro_out), (co, co_out)))]
     for k in range(kinds):
         factor = ai[k] * coef[k:k + 1, :]
         for c in range(2):

time: 32.3 us -> 32.2 us (level)
  no operation moved by 1% of the time
where the time goes in v6:
time: 32.2 us; the launch traced here: 32.1 us
  Pallas kernels  31.4 us (98%)
  between operations  0.65 us (2%)
    pallas_call x1, Pallas kernels, local_step(): pl.pallas_call(lambda *refs: grads_kernel(n, *refs), out_shape=[pltpu.VME...  28 us
    pallas_call x1, Pallas kernels, local_step(): pl.pallas_call(apply_kernel, out_shape=[jax.ShapeDtypeStruct(s, F32) for...  2.03 us
    pallas_call x1, Pallas kernels, local_step(): pl.pallas_call(lambda *refs: scalar_kernel(kinds + 1 + 2 * i, *refs), out...  1.37 us

profile of v6, /device:TPU:0, one launch (start us, length us, event | category | flops | bytes accessed | tf_op | source)
XLA Modules:
  0.0 32.1 jit_solution(1498797408996668223)
XLA Ops:
  0.6 1.4 %conditional.1 = (f32[8,128]{1,0:T(8,128)S(1)}) conditional(s32[]{:T(128)} %clamp.3, (f32[]{:T(128)}, f32[]{:T(128)}) %tuple.17, (f32[]{:T(128)}, f32[]{:T(128)}) %tuple.18, () %tuple.19), branch_computations={%region_0.0_spmd, %region_1.0_spmd, %region_2.0_spmd} | conditional | bytes 4108 | solution.py:440
  0.6 1.4 %scalar.2 = f32[8,128]{1,0:T(8,128)S(1)} custom-call(f32[1,1]{1,0:T(1,128)} %bitcast.refs_0_, f32[1,1]{1,0:T(1,128)} %bitcast.1.refs_1_), custom_call_target="tpu_custom_call" | custom-call | tf_op jit(solution)/shard_map/cond/branch_0_fun/scalar/pallas_call | solution.py:442
  2.0 28.0 %grads.1 = (f32[10,2,64,512]{3,2,1,0:T(8,128)S(1)}, f32[2,2,160,512]{3,2,1,0:T(8,128)S(1)}, f32[2,64,5120]{2,1,0:T(8,128)S(1)}, f32[160,2048]{1,0:T(8,128)S(1)},...) custom-call(bf16[64,4096]{1,0:T(8,128)(2,1)} %bitcast.11, ...), custom_call_target="tpu_custom_call" | custom-call | tf_op jit(solution)/shard_map/grads/pallas_call | solution.py:465
  30.0 2.0 %apply.1 = (f32[2,64,5120]{2,1,0:T(8,128)}, f32[2,64]{1,0:T(2,128)}, f32[2,5120]{1,0:T(2,128)}, f32[160,2048]{1,0:T(8,128)}, f32[1,160]{1,0:T(1,128)}, /*index=5*/f32[16,128]{1,0:T(8,128)}) custom-call(f32[10,2,64,512]{3,2,1,0:T(8,128)S(1)} %get-tuple-element.40.gi, f32[2,2,160,512]{3,2,1,0:T(8,128)S(1)} %get-tuple-element.41.go, ...), custom_call_target="tpu_custom_call" | custom-call | tf_op jit(solution)/shard_map/apply/pallas_call | solution.py:475

commit v7 on v6

--- a/solution.py
+++ b/solution.py
@@ -21,7 +21,7 @@
                  gi, go, wi, wo, ri_new, ci_new, ro_new, co_new, coef, ai, ao, colf,
                  xs, hs, dy, si, so, csend, land, mid_land, misc_land, last_land, csum, ri_sq, ro_sq, ri_got, ro_got, split,
                  fsend, f_land, ri, ci, ro, co, scal,
-                 dy_sem, w_sem, xs_sem, g_sem, land_sem, mid_sem, misc_sem, last_sem, fwd_sem, row_sem, f_sem):
+                 dy_sem, xs_sem, g_sem, land_sem, mid_sem, misc_sem, last_sem, fwd_sem, row_sem, f_sem):
     me = lax.axis_index('tp')
     core = lax.rem(me, 2)
     chip = me // 2
@@ -79,8 +79,8 @@
         return pltpu.make_async_copy(dyi_hbm.at[t // per_in, some, cols], dy.at[slot, some, :], dy_sem.at[(t + part) % AHEAD])
 
     barrier = pltpu.get_barrier_semaphore()
-    x_copy = pltpu.make_async_copy(x_hbm, xs.at[pl.ds(0, m_in)], w_sem.at[0])
-    h_copy = pltpu.make_async_copy(h_hbm, hs.at[pl.ds(0, m_out)], w_sem.at[1])
+    x_copy = pltpu.make_async_copy(x_hbm, xs.at[pl.ds(0, m_in)], xs_sem.at[0, 0])
+    h_copy = pltpu.make_async_copy(h_hbm, hs.at[pl.ds(0, m_out)], xs_sem.at[1, 0])
     x_copy.start()
     h_copy.start()
     out_copy(0).start()
@@ -221,8 +221,10 @@
         some = pl.ds(part * (tokens // PARTS), tokens // PARTS)
         last_copy(part).wait()
         if part == PARTS - 1:
-            wi_copy = pltpu.make_async_copy(wi_hbm, wi, w_sem.at[0])
-            wo_copy = pltpu.make_async_copy(wo_hbm, wo, w_sem.at[1])
+            x_send.wait_send()
+            h_send.wait_send()
+            wi_copy = pltpu.make_async_copy(wi_hbm, wi, xs_sem.at[0, 0])
+            wo_copy = pltpu.make_async_copy(wo_hbm, wo, xs_sem.at[1, 0])
             wi_copy.start()
             wo_copy.start()
         for h in range(2):
@@ -366,8 +368,6 @@
         else:
             ri_new[i:i + 1, :] = flat
 
-    x_send.wait_send()
-    h_send.wait_send()
     forward.wait_send()
     wait_for(so, g_sem.at[0, 0])
     wait_for(si, g_sem.at[1, 0])
@@ -460,7 +460,7 @@
                 ((1, LANES), F32), ((n, 1, LANES), F32),
                 (row_in.shape, F32), (col_in.shape, F32), ((1, m_out), F32), ((cols_out // LANES, LANES), F32)]
         vmem.append(((8, LANES), F32))
-        sems = [(AHEAD,), (2,), (2, 2), (2, 2), (2,), (2,), (2,), (2,), (2,), (2, 2), (2,)]
+        sems = [(AHEAD,), (2, 2), (2, 2), (2,), (2,), (2,), (2,), (2,), (2, 2), (2,)]
         anywhere = pl.BlockSpec(memory_space=pl.ANY)
         mid = pl.pallas_call(
             lambda *refs: grads_kernel(n, *refs),

time: 32.2 us -> 32.2 us (level)
  no operation moved by 1% of the time
where the time goes in v7:
time: 32.2 us; the launch traced here: 32 us
  Pallas kernels  31.4 us (98%)
  between operations  0.65 us (2%)
    pallas_call x1, Pallas kernels, local_step(): pl.pallas_call(lambda *refs: grads_kernel(n, *refs), out_shape=[pltpu.VME...  28 us
    pallas_call x1, Pallas kernels, local_step(): pl.pallas_call(apply_kernel, out_shape=[jax.ShapeDtypeStruct(s, F32) for...  2.03 us
    pallas_call x1, Pallas kernels, local_step(): pl.pallas_call(lambda *refs: scalar_kernel(kinds + 1 + 2 * i, *refs), out...  1.37 us

profile of v7, /device:TPU:0, one launch (start us, length us, event | category | flops | bytes accessed | tf_op | source)
XLA Modules:
  0.0 32.0 jit_solution(15219551768815060657)
XLA Ops:
  0.6 1.4 %conditional.1 = (f32[8,128]{1,0:T(8,128)S(1)}) conditional(s32[]{:T(128)} %clamp.3, (f32[]{:T(128)}, f32[]{:T(128)}) %tuple.17, (f32[]{:T(128)}, f32[]{:T(128)}) %tuple.18, () %tuple.19), branch_computations={%region_0.0_spmd, %region_1.0_spmd, %region_2.0_spmd} | conditional | bytes 4108 | solution.py:440
  0.6 1.4 %scalar.2 = f32[8,128]{1,0:T(8,128)S(1)} custom-call(f32[1,1]{1,0:T(1,128)} %bitcast.refs_0_, f32[1,1]{1,0:T(1,128)} %bitcast.1.refs_1_), custom_call_target="tpu_custom_call" | custom-call | tf_op jit(solution)/shard_map/cond/branch_0_fun/scalar/pallas_call | solution.py:442
  2.0 28.0 %grads.1 = (f32[10,2,64,512]{3,2,1,0:T(8,128)S(1)}, f32[2,2,160,512]{3,2,1,0:T(8,128)S(1)}, f32[2,64,5120]{2,1,0:T(8,128)S(1)}, f32[160,2048]{1,0:T(8,128)S(1)},...) custom-call(bf16[64,4096]{1,0:T(8,128)(2,1)} %bitcast.11, ...), custom_call_target="tpu_custom_call" | custom-call | tf_op jit(solution)/shard_map/grads/pallas_call | solution.py:465
  30.0 2.0 %apply.1 = (f32[2,64,5120]{2,1,0:T(8,128)}, f32[2,64]{1,0:T(2,128)}, f32[2,5120]{1,0:T(2,128)}, f32[160,2048]{1,0:T(8,128)}, f32[1,160]{1,0:T(1,128)}, /*index=5*/f32[16,128]{1,0:T(8,128)}) custom-call(f32[10,2,64,512]{3,2,1,0:T(8,128)S(1)} %get-tuple-element.40.gi, f32[2,2,160,512]{3,2,1,0:T(8,128)S(1)} %get-tuple-element.41.go, ...), custom_call_target="tpu_custom_call" | custom-call | tf_op jit(solution)/shard_map/apply/pallas_call | solution.py:475
